TPU v7x, 32 devices: a whole 2x2x4 slice. The times are simulated.
32 devices in a mesh: strip: 8 (over z, x), seq: 4 (over y, core).
Axes of the slice: x: 2, y: 2, z: 4, core: 2. Of those that a mesh axis runs over, the one named last changes fastest.
Arguments:
- patches: bfloat16 [32, 536, 768], P('strip', 'seq'), may hold values from -6 to 6
- lengths: int32 [32], P('strip'), may hold values from 1 to 536, as said below
- script: int32 [32], P('strip'), may hold values from 0 to 3, as said below
- script_table: bfloat16 [4, 768], replicated, may hold values from -3 to 3
- gain_one: float32 [768], replicated, may hold values from 0.25 to 1.75
- bias_one: float32 [768], replicated, may hold values from -2 to 2
- qkv_weight: bfloat16 [768, 2304], replicated, may hold values from -0.3125 to 0.3125
- query_bias: float32 [768], replicated, may hold values from -3 to 3
- value_bias: float32 [768], replicated, may hold values from -3 to 3
- out_weight: bfloat16 [768, 768], replicated, may hold values from -0.875 to 0.875
- out_bias: float32 [768], replicated, may hold values from -3 to 3
- gain_two: float32 [768], replicated, may hold values from 0.25 to 1.75
- bias_two: float32 [768], replicated, may hold values from -2 to 2
- up_weight: bfloat16 [768, 3072], replicated, may hold values from -0.21875 to 0.21875
- up_bias: float32 [3072], replicated, may hold values from -3 to 3
- down_weight: bfloat16 [3072, 768], replicated, may hold values from -0.109375 to 0.109375
- down_bias: float32 [768], replicated, may hold values from -3 to 3
- cotangent: bfloat16 [32, 536, 768], P('strip', 'seq'), may hold values from -6 to 6
Outputs:
- layer_out: bfloat16 [32, 536, 768], P('strip', 'seq')
- grad_patches: bfloat16 [32, 536, 768], P('strip', 'seq')
- grad_table: float32 [768, 4], P(('strip', 'seq'))
- grad_gain_one: float32 [768], P(('strip', 'seq'))
- grad_bias_one: float32 [768], P(('strip', 'seq'))
- grad_qkv: float32 [768, 2304], P(('strip', 'seq'))
- grad_query_bias: float32 [768], P(('strip', 'seq'))
- grad_value_bias: float32 [768], P(('strip', 'seq'))
- grad_out_weight: float32 [768, 768], P(('strip', 'seq'))
- grad_out_bias: float32 [768], P(('strip', 'seq'))
- grad_gain_two: float32 [768], P(('strip', 'seq'))
- grad_bias_two: float32 [768], P(('strip', 'seq'))
- grad_up_weight: float32 [768, 3072], P(('strip', 'seq'))
- grad_up_bias: float32 [3072], P(('strip', 'seq'))
- grad_down_weight: float32 [3072, 768], P(('strip', 'seq'))
- grad_down_bias: float32 [768], P(('strip', 'seq'))
Inputs may be any that keep to these rules, and one draw needn't show every extreme that they name: The first lengths[s] patch slots of strip s are filled; some strip has all 536 filled. `script`: script ids never fall from one strip to the next.
All inputs are finite; a program needn't handle non-finite values.
Results may differ from a plain program's by a relative error of at most 0.013.
The roundings to bfloat16 on the way count: a program that leaves them out, or rounds other values in their place, can miss the bound.
Values may be sent and summed in bfloat16 or wider, within the bound.
A program may use at most 192 MiB of HBM per device.

v0:
```python
import jax
import jax.numpy as jnp
from jax import lax
from jax.sharding import PartitionSpec as P

HD = 64


epsilon = 1e-12


def normalize(hidden):
    centred = hidden - jnp.mean(hidden, axis=-1, keepdims=True)
    inverse = lax.rsqrt(jnp.mean(centred * centred, axis=-1, keepdims=True) + epsilon)
    return (centred * inverse, inverse)


def norm_back(upstream, gain, normed, inverse):
    scaled = upstream * gain
    return inverse * (
        scaled
        - jnp.mean(scaled, axis=-1, keepdims=True)
        - normed * jnp.mean(scaled * normed, axis=-1, keepdims=True)
    )


def weight_grad(inputs, upstream):
    return lax.dot_general(
        inputs, upstream, (((0,), (0,)), ((), ())), preferred_element_type=jnp.float32
    )


def input_grad(upstream, weight):
    return lax.dot_general(
        upstream, weight, (((1,), (1,)), ((), ())), preferred_element_type=jnp.float32
    )


def gelu_slope(upper):
    return (
        0.5 * (1.0 + lax.erf(upper * 0.7071067811865476))
        + upper * jnp.exp(-0.5 * upper * upper) * 0.3989422804014327
    )


def split_block(block):
    seq_len = block.shape[0]
    heads_here = block.shape[2] // HD
    return [block[:, member].reshape(seq_len, heads_here, HD) for member in range(3)]


def masked_logits(queries, key_rows, length):
    logits = jnp.einsum(
        "qhd,khd->hqk", queries, key_rows, preferred_element_type=jnp.float32
    ) * HD ** (-0.5)
    visible = jnp.arange(logits.shape[-1], dtype=jnp.int32) < length
    return jnp.where(visible[None, None, :], logits, -1000000000.0)


def attend_forward(item):
    block, length = item
    queries, key_rows, values = split_block(block)
    logits = masked_logits(queries, key_rows, length)
    highest = jnp.max(logits, axis=-1, keepdims=True)
    expanded = jnp.exp(logits - highest)
    totals = jnp.sum(expanded, axis=-1, keepdims=True)
    probs = (expanded / totals).astype(jnp.bfloat16)
    mixed = jnp.einsum("hqk,khd->qhd", probs, values, preferred_element_type=jnp.float32)
    mixed = mixed.astype(jnp.bfloat16).reshape(block.shape[0], block.shape[2])
    return (mixed, (highest + jnp.log(totals))[..., 0])


def attend_backward(item):
    block, log_total, grad_mixed, length = item
    queries, key_rows, values = split_block(block)
    logits = masked_logits(queries, key_rows, length)
    probs = jnp.exp(logits - log_total[..., None])
    grad_heads = grad_mixed.reshape(queries.shape)
    grad_values = jnp.einsum(
        "hqk,qhd->khd", probs.astype(jnp.bfloat16), grad_heads, preferred_element_type=jnp.float32
    )
    grad_probs = jnp.einsum("qhd,khd->hqk", grad_heads, values, preferred_element_type=jnp.float32)
    inner = jnp.sum(probs * grad_probs, axis=-1, keepdims=True)
    grad_logits = (probs * (grad_probs - inner)).astype(jnp.bfloat16)
    grad_queries = jnp.einsum(
        "hqk,khd->qhd", grad_logits, key_rows, preferred_element_type=jnp.float32
    ) * HD ** (-0.5)
    grad_keys = jnp.einsum(
        "hqk,qhd->khd", grad_logits, queries, preferred_element_type=jnp.float32
    ) * HD ** (-0.5)
    stacked = jnp.stack([grad_queries, grad_keys, grad_values], axis=1)
    return stacked.reshape(block.shape).astype(jnp.bfloat16)


def local(
    patches,
    lengths,
    script,
    script_table,
    gain_one,
    bias_one,
    qkv_weight,
    query_bias,
    value_bias,
    out_weight,
    out_bias,
    gain_two,
    bias_two,
    up_weight,
    up_bias,
    down_weight,
    down_bias,
    cotangent,
):
    strips, row_count, model_width = patches.shape
    groups = script_table.shape[0]
    tokens = strips * row_count
    selector = (script[:, None] == jnp.arange(groups, dtype=jnp.int32)[None, :]).astype(jnp.float32)
    added = jnp.dot(selector.astype(jnp.bfloat16), script_table, preferred_element_type=jnp.float32)
    hidden = (patches.astype(jnp.float32) + added[:, None, :]).reshape(tokens, model_width)
    normed_one, inverse_one = normalize(hidden)
    inputs_one = (normed_one * gain_one + bias_one).astype(jnp.bfloat16)
    joint_bias = jnp.concatenate([query_bias, jnp.zeros_like(query_bias), value_bias])
    projected = (
        jnp.dot(inputs_one, qkv_weight, preferred_element_type=jnp.float32) + joint_bias
    ).astype(jnp.bfloat16)
    projected = projected.reshape(strips, row_count, 3, model_width)
    head_blocks = lax.all_to_all(projected, "seq", split_axis=3, concat_axis=1, tiled=True)
    mixed_heads, log_totals = lax.map(attend_forward, (head_blocks, lengths))
    mixed = lax.all_to_all(mixed_heads, "seq", split_axis=1, concat_axis=2, tiled=True).reshape(
        tokens, model_width
    )
    attended = hidden + jnp.dot(mixed, out_weight, preferred_element_type=jnp.float32) + out_bias
    normed_two, inverse_two = normalize(attended)
    inputs_two = (normed_two * gain_two + bias_two).astype(jnp.bfloat16)
    upper = jnp.dot(inputs_two, up_weight, preferred_element_type=jnp.float32) + up_bias
    active = jax.nn.gelu(upper, approximate=False).astype(jnp.bfloat16)
    result = attended + jnp.dot(active, down_weight, preferred_element_type=jnp.float32) + down_bias
    layer_out = result.astype(jnp.bfloat16).reshape(strips, row_count, model_width)
    grad_result = cotangent.reshape(tokens, model_width)
    grad_float = grad_result.astype(jnp.float32)
    grad_down_weight = weight_grad(active, grad_result)
    grad_down_bias = jnp.sum(grad_float, axis=0)
    grad_upper = (input_grad(grad_result, down_weight) * gelu_slope(upper)).astype(jnp.bfloat16)
    grad_up_weight = weight_grad(inputs_two, grad_upper)
    grad_up_bias = jnp.sum(grad_upper.astype(jnp.float32), axis=0)
    grad_inputs_two = input_grad(grad_upper, up_weight)
    grad_gain_two = jnp.sum(grad_inputs_two * normed_two, axis=0)
    grad_bias_two = jnp.sum(grad_inputs_two, axis=0)
    grad_attended = grad_float + norm_back(grad_inputs_two, gain_two, normed_two, inverse_two)
    grad_branch = grad_attended.astype(jnp.bfloat16)
    grad_out_weight = weight_grad(mixed, grad_branch)
    grad_out_bias = jnp.sum(grad_branch.astype(jnp.float32), axis=0)
    grad_mixed = (
        input_grad(grad_branch, out_weight)
        .astype(jnp.bfloat16)
        .reshape(strips, row_count, model_width)
    )
    grad_mixed_heads = lax.all_to_all(grad_mixed, "seq", split_axis=2, concat_axis=1, tiled=True)
    grad_heads = lax.map(attend_backward, (head_blocks, log_totals, grad_mixed_heads, lengths))
    grad_projected = lax.all_to_all(
        grad_heads, "seq", split_axis=1, concat_axis=3, tiled=True
    ).reshape(tokens, 3 * model_width)
    grad_qkv = weight_grad(inputs_one, grad_projected)
    grad_bias_rows = jnp.sum(grad_projected.astype(jnp.float32), axis=0)
    grad_query_bias = grad_bias_rows[:model_width]
    grad_value_bias = grad_bias_rows[2 * model_width :]
    grad_inputs_one = input_grad(grad_projected, qkv_weight)
    grad_gain_one = jnp.sum(grad_inputs_one * normed_one, axis=0)
    grad_bias_one = jnp.sum(grad_inputs_one, axis=0)
    grad_hidden = grad_attended + norm_back(grad_inputs_one, gain_one, normed_one, inverse_one)
    grad_patches = grad_hidden.astype(jnp.bfloat16).reshape(strips, row_count, model_width)
    per_strip = jnp.sum(grad_hidden.reshape(strips, row_count, model_width), axis=1)
    grad_table = jnp.dot(per_strip.T, selector, precision=lax.Precision.HIGHEST)
    summed = (
        lax.psum_scatter(grad_table, ("strip", "seq"), scatter_dimension=0, tiled=True),
        lax.psum_scatter(grad_gain_one, ("strip", "seq"), scatter_dimension=0, tiled=True),
        lax.psum_scatter(grad_bias_one, ("strip", "seq"), scatter_dimension=0, tiled=True),
        lax.psum_scatter(grad_qkv, ("strip", "seq"), scatter_dimension=0, tiled=True),
        lax.psum_scatter(grad_query_bias, ("strip", "seq"), scatter_dimension=0, tiled=True),
        lax.psum_scatter(grad_value_bias, ("strip", "seq"), scatter_dimension=0, tiled=True),
        lax.psum_scatter(grad_out_weight, ("strip", "seq"), scatter_dimension=0, tiled=True),
        lax.psum_scatter(grad_out_bias, ("strip", "seq"), scatter_dimension=0, tiled=True),
        lax.psum_scatter(grad_gain_two, ("strip", "seq"), scatter_dimension=0, tiled=True),
        lax.psum_scatter(grad_bias_two, ("strip", "seq"), scatter_dimension=0, tiled=True),
        lax.psum_scatter(grad_up_weight, ("strip", "seq"), scatter_dimension=0, tiled=True),
        lax.psum_scatter(grad_up_bias, ("strip", "seq"), scatter_dimension=0, tiled=True),
        lax.psum_scatter(grad_down_weight, ("strip", "seq"), scatter_dimension=0, tiled=True),
        lax.psum_scatter(grad_down_bias, ("strip", "seq"), scatter_dimension=0, tiled=True),
    )
    return (
        layer_out,
        grad_patches,
        summed[0],
        summed[1],
        summed[2],
        summed[3],
        summed[4],
        summed[5],
        summed[6],
        summed[7],
        summed[8],
        summed[9],
        summed[10],
        summed[11],
        summed[12],
        summed[13],
    )


def solution(mesh):
    placed = (
        P("strip", "seq", None),
        P("strip"),
        P("strip"),
        P(),
        P(),
        P(),
        P(),
        P(),
        P(),
        P(),
        P(),
        P(),
        P(),
        P(),
        P(),
        P(),
        P(),
        P("strip", "seq", None),
    )
    return jax.shard_map(
        local,
        mesh=mesh,
        in_specs=placed,
        out_specs=(
            P("strip", "seq", None),
            P("strip", "seq", None),
            P(("strip", "seq"), None),
            P(("strip", "seq")),
            P(("strip", "seq")),
            P(("strip", "seq"), None),
            P(("strip", "seq")),
            P(("strip", "seq")),
            P(("strip", "seq"), None),
            P(("strip", "seq")),
            P(("strip", "seq")),
            P(("strip", "seq")),
            P(("strip", "seq"), None),
            P(("strip", "seq")),
            P(("strip", "seq"), None),
            P(("strip", "seq")),
        ),
        check_vma=False,
    )
```

profile of v0, /device:TPU:0, one launch (start us, length us, event | category | flops | bytes accessed | tf_op | source)
XLA Modules:
  0.0 786.1 jit_solution(12835965384405361480)
XLA Ops:
  10.6 2.6 multiply_reduce_fusion.6
  17.2 3.0 add_convert_fusion.1
  21.7 2.8 reshape.248
  25.4 5.2 add_convert_fusion
  30.5 7.7 reshape.249
  38.3 10.1 %copy.125 = bf16[4,134,3,768]{1,0,2,3:T(4,128)(2,1)} copy(bf16[4,134,3,768]{3,2,1,0:T(4,128)(2,1)} %reshape.249) | data formatting | bytes 4939776 | tf_op jit(solution)/shard_map/reshape | solution.py:127
  48.4 5.1 all-to-all-start
  53.5 54.5 %all-to-all-done = bf16[4,134,3,768]{1,0,2,3:T(4,128)(2,1)} async-done(((bf16[4,134,3,768]{1,0,2,3:T(4,128)(2,1)}), bf16[4,134,3,768]{1,0,2,3:T(4,128)(2,1)}, u32[]{:S(2)}, u32[]{:S(2)}) %all-to-all-start) | async-done | bytes 2469920 | tf_op jit(solution)/shard_map/all_to_all | solution.py:128
  108.0 8.1 %copy.158 = bf16[4,4,134,3,192]{2,1,4,3,0:T(4,128)(2,1)} copy(bf16[4,4,134,3,192]{2,0,3,4,1:T(4,128)(2,1)} %bitcast.23) | data formatting | bytes 4939776 | tf_op jit(solution)/shard_map/while | solution.py:129
  116.2 8.7 %reshape.260 = bf16[4,536,3,192]{1,3,2,0:T(8,128)(2,1)} reshape(bf16[4,4,134,3,192]{2,1,4,3,0:T(4,128)(2,1)} %copy.158) | data formatting | bytes 4939776 | tf_op jit(solution)/shard_map/while | solution.py:129
  124.9 27.9 %while.22 = (s32[]{:T(128)}, bf16[4,536,192]{1,2,0:T(8,128)(2,1)}, f32[4,3,536]{2,1,0:T(4,128)}, bf16[4,536,3,192]{1,3,2,0:T(8,128)(2,1)}, s32[4]{0:T(128)S(1)}, /*index=5*/s32[]{:T(128)}) while((s32[]{:T(128)}, bf16[4,536,192]{1,2,0:T(8,128)(2,1)}, f32[4,3,536]{2,1,0:T(4,128)}, bf16[4,536,3,192]{1,3,2,0:T(8,128)(2,1)}, s32[4]{0:T(128)S(1)}, ...), condition=%wide.region_5.6_spmd, body=%wide.region_2.5_spmd.sunk | while | flops 231087808 | bytes 14145945 | solution.py:129
  152.8 3.3 copy.129
  156.0 4.5 all-to-all-start.1
  162.7 2.3 reshape.252
  164.9 10.6 %all-to-all-done.1 = bf16[4,536,192]{2,0,1:T(4,128)(2,1)} async-done(((bf16[4,536,192]{2,0,1:T(4,128)(2,1)}), bf16[4,536,192]{2,0,1:T(4,128)(2,1)}, u32[]{:S(2)}, u32[]{:S(2)}) %all-to-all-start.1) | async-done | bytes 823328 | tf_op jit(solution)/shard_map/all_to_all | solution.py:130
  178.3 3.1 reshape.250
  181.4 3.1 fusion.51
  184.9 20.2 %fusion.19 = (bf16[536,3072]{1,0:T(8,128)(2,1)}, f32[536,3072]{1,0:T(8,128)S(1)}) fusion(f32[3072]{0:T(1024)S(1)} %copy-done.19, bf16[768,3072]{1,0:T(8,128)(2,1)} %param.35, f32[536,768]{1,0:T(8,128)S(1)} %get-tuple-element.262, f32[768]{0:T(1024)S(1)} %copy-done.9, f32[768]{0:T(1024)S(1)} %copy-done.8, f32[536]{0:T(1024)S(1)} %add_rsqrt_fusion.1, ...), kind=kOutput, calls=%fused_computation.36 | convolution fusion | flops 2639898624 | bytes 16267456 | tf_op jit(solution)/shard_map/dot_general | solution.py:136
  205.2 5.9 convert_reduce_fusion.1
  211.0 3.7 multiply_reduce_fusion.1
  221.2 3.5 copy.133
  224.7 4.4 all-to-all-start.2
  229.2 4.2 fusion.42
  233.4 15.8 %all-to-all-done.2 = bf16[4,134,768]{1,0,2:T(4,128)(2,1)} async-done(((bf16[4,134,768]{1,0,2:T(4,128)(2,1)}), bf16[4,134,768]{1,0,2:T(4,128)(2,1)}, u32[]{:S(2)}, u32[]{:S(2)}) %all-to-all-start.2) | async-done | bytes 823328 | tf_op jit(solution)/shard_map/all_to_all | solution.py:159
  249.2 3.9 copy.154
  253.1 4.1 reshape.257
  257.1 45.3 %while.23 = (s32[]{:T(128)}, bf16[4,536,3,192]{1,3,2,0:T(8,128)(2,1)}, bf16[4,536,3,192]{1,3,2,0:T(8,128)(2,1)}, s32[4]{0:T(128)}, f32[4,3,536]{2,1,0:T(4,128)}, /*index=5*/bf16[4,536,192]{1,2,0:T(8,128)(2,1)}, s32[]{:T(128)}) while((s32[]{:T(128)}, bf16[4,536,3,192]{1,3,2,0:T(8,128)(2,1)}, bf16[4,536,3,192]{1,3,2,0:T(8,128)(2,1)}, ...), condition=%wide.region_12.13_spmd, body=%wide.region_10.12_spmd.sunk | while | flops 566902528 | bytes 32199044 | solution.py:160
  302.4 7.7 copy.138
  310.0 4.7 all-to-all-start.3
  319.2 34.6 %all-to-all-done.3 = bf16[4,536,3,192]{3,0,2,1:T(4,128)(2,1)} async-done(((bf16[4,536,3,192]{3,0,2,1:T(4,128)(2,1)}), bf16[4,536,3,192]{3,0,2,1:T(4,128)(2,1)}, u32[]{:S(2)}, u32[]{:S(2)}) %all-to-all-start.3) | async-done | bytes 2469920 | tf_op jit(solution)/shard_map/all_to_all | solution.py:161
  353.8 2.4 copy.167
  356.3 3.0 copy.140
  359.2 6.8 reshape.254
  366.0 7.8 fusion.53
  373.9 10.2 %fusion.45 = f32[768,3072]{1,0:T(8,128)} fusion(bf16[536,3072]{1,0:T(8,128)(2,1)} %copy-done.6, f32[536,768]{1,0:T(8,128)} %copy-done.3, f32[768]{0:T(1024)S(1)} %copy-done.9, f32[768]{0:T(1024)S(1)} %copy-done.8, f32[536]{0:T(1024)S(1)} %add_rsqrt_fusion.1, f32[536]{0:T(1024)S(1)} %broadcast_multiply_fusion.5), kind=kOutput, calls=%fused_computation.107 | convolution fusion | flops 2531223552 | bytes 14387392 | tf_op jit(solution)/shard_map/dot_general | solution.py:28
  384.4 9.9 %fusion.54 = f32[3072,768]{1,0:T(8,128)} fusion(bf16[536,3072]{1,0:T(8,128)(2,1)} %get-tuple-element.263, bf16[536,768]{1,0:T(8,128)(2,1)} %reshape.252), kind=kOutput, calls=%fused_computation.116 | convolution fusion | flops 2529165312 | bytes 13553664 | tf_op jit(solution)/shard_map/dot_general | solution.py:28
  395.9 7.7 add_convert_fusion.2
  403.6 2.3 reshape.251
  405.9 2.4 copy.143
  408.3 5.5 multiply_reduce_fusion.2
  415.9 2.8 reshape.256
  420.9 2.4 convert_reduce_fusion
  426.3 44.2 %all-reduce.10 = (f32[768,4]{0,1:T(4,128)}, f32[768]{0:T(1024)}, f32[768]{0:T(1024)}, f32[768]{0:T(1024)}, f32[768]{0:T(1024)}, /*index=5*/f32[768]{0:T(1024)}, ...) all-reduce(f32[768,4]{0,1:T(4,128)} %fusion.38, ...), channel_id=2, replica_groups=mesh['strip'=8,'seq'=4] {'strip','seq'}, use_global_device_ids=true, to_apply=%region_16.17.clone | all-reduce | flops 12288 | bytes 98304
  480.6 2.3 reshape.255
  482.9 2.4 copy.144
  487.8 8.3 %reduce-scatter.6.cloned.1.call-done = f32[24,2304]{1,0:T(8,128)} async-done(((f32[768,2304]{1,0:T(8,128)}), f32[24,2304]{1,0:T(8,128)}) %reduce-scatter.6.cloned.1.call-update) | async-done | bytes 221200 | tf_op jit(solution)/shard_map/reduce_scatter | solution.py:179
  496.1 141.7 %reduce-scatter.10.cloned.1.call-done = f32[24,3072]{1,0:T(8,128)} async-done(((f32[768,3072]{1,0:T(8,128)}), f32[24,3072]{1,0:T(8,128)}) %reduce-scatter.10.cloned.1.call-update) | async-done | bytes 294928 | tf_op jit(solution)/shard_map/reduce_scatter | solution.py:186
  637.8 141.5 %reduce-scatter.12.cloned.1.call-done = f32[96,768]{1,0:T(8,128)} async-done(((f32[3072,768]{1,0:T(8,128)}), f32[96,768]{1,0:T(8,128)}) %reduce-scatter.12.cloned.1.call-update) | async-done | bytes 294928 | tf_op jit(solution)/shard_map/reduce_scatter | solution.py:188
  (204 shorter events, 120.8 us)
Async XLA Ops:
  7.2 18.2 %copy-start = (bf16[768,2304]{1,0:T(8,128)(2,1)S(1)}, bf16[768,2304]{1,0:T(8,128)(2,1)}, u32[]{:S(2)}) copy-start(bf16[768,2304]{1,0:T(8,128)(2,1)} %param.28) | copy-start | bytes 10616836
  9.9 0.6 copy-start.7
  20.2 4.3 copy-start.17
  20.2 5.2 copy-start.10
  24.6 6.0 copy-start.13
  24.6 5.9 copy-start.15
  48.4 59.6 %all-to-all-start = ((bf16[4,134,3,768]{1,0,2,3:T(4,128)(2,1)}), bf16[4,134,3,768]{1,0,2,3:T(4,128)(2,1)}, u32[]{:S(2)}, u32[]{:S(2)}) async-start(bf16[4,134,3,768]{1,0,2,3:T(4,128)(2,1)} %copy.125), calls=%async_computation | async-start | bytes 9437184 | tf_op jit(solution)/shard_map/all_to_all | solution.py:128
  116.1 8.7 %copy-start.21 = (s32[4]{0:T(128)S(1)}, s32[4]{0:T(128)}, u32[]{:S(2)}) copy-start(s32[4]{0:T(128)} %param.23) | copy-start | bytes 52
  156.0 19.5 %all-to-all-start.1 = ((bf16[4,536,192]{2,0,1:T(4,128)(2,1)}), bf16[4,536,192]{2,0,1:T(4,128)(2,1)}, u32[]{:S(2)}, u32[]{:S(2)}) async-start(bf16[4,536,192]{2,0,1:T(4,128)(2,1)} %copy.129), calls=%async_computation.1 | async-start | bytes 2195456 | tf_op jit(solution)/shard_map/all_to_all | solution.py:130
  164.9 16.4 %copy-start.20 = (f32[768]{0:T(1024)S(1)}, f32[768]{0:T(1024)}, u32[]{:S(2)}) copy-start(f32[768]{0:T(1024)} %param.32) | copy-start | bytes 9220
  181.3 3.5 copy-start.8
  181.3 3.5 copy-start.9
  181.3 3.5 copy-start.19
  181.4 23.8 %slice-start.2 = ((s8[4718592]{0:T(1024)(128)(4,1)}), s8[4194304]{0:T(1024)(128)(4,1)S(1)}, s32[]{:S(2)}) async-start(s8[4718592]{0:T(1024)(128)(4,1)} %bitcast.162), calls=%async_computation.14 | async-start | bytes 8388608
  181.4 29.7 %slice-start = ((s8[4718592]{0:T(1024)(128)(4,1)}), s8[4194304]{0:T(1024)(128)(4,1)S(1)}, s32[]{:S(2)}) async-start(s8[4718592]{0:T(1024)(128)(4,1)} %bitcast.160), calls=%async_computation.12 | async-start | bytes 8388608
  184.5 30.2 %copy-start.3 = (f32[536,768]{1,0:T(8,128)}, f32[536,768]{1,0:T(8,128)S(1)}, u32[]{:S(2)}) copy-start(f32[536,768]{1,0:T(8,128)S(1)} %get-tuple-element.262) | copy-start | bytes 4939780
  184.9 20.2 %copy-start.5 = (bf16[536,768]{1,0:T(8,128)(2,1)S(1)}, bf16[536,768]{1,0:T(8,128)(2,1)}, u32[]{:S(2)}) copy-start(bf16[536,768]{1,0:T(8,128)(2,1)} %reshape.252) | copy-start | bytes 2469892
  184.9 20.2 %slice-start.3 = ((s8[4718592]{0:T(1024)(128)(4,1)}), s8[524288]{0:T(1024)(128)(4,1)S(1)}, s32[]{:S(2)}) async-start(s8[4718592]{0:T(1024)(128)(4,1)} %bitcast.162), calls=%async_computation.15 | async-start | bytes 1048576
  184.9 26.1 %slice-start.1 = ((s8[4718592]{0:T(1024)(128)(4,1)}), s8[524288]{0:T(1024)(128)(4,1)S(1)}, s32[]{:S(2)}) async-start(s8[4718592]{0:T(1024)(128)(4,1)} %bitcast.160), calls=%async_computation.13 | async-start | bytes 1048576
  211.0 3.7 copy-start.6
  214.7 2.5 copy-start.18
  216.0 1.2 copy-start.1
  224.7 24.5 %all-to-all-start.2 = ((bf16[4,134,768]{1,0,2:T(4,128)(2,1)}), bf16[4,134,768]{1,0,2:T(4,128)(2,1)}, u32[]{:S(2)}, u32[]{:S(2)}) async-start(bf16[4,134,768]{1,0,2:T(4,128)(2,1)} %copy.133), calls=%async_computation.2 | async-start | bytes 3145728 | tf_op jit(solution)/shard_map/all_to_all | solution.py:159
  229.1 258.7 %reduce-scatter.8.cloned.1.call-start = ((), (), s32[]{:S(2)}) async-start(), calls=%async_computation.9 | async-start | bytes 2433024 | tf_op jit(solution)/shard_map/reduce_scatter | solution.py:182
  258.3 1.6 copy-start.22
  269.6 1.6 copy-start.22
  280.9 1.6 copy-start.22
  292.2 1.6 copy-start.22
  310.0 43.8 %all-to-all-start.3 = ((bf16[4,536,3,192]{3,0,2,1:T(4,128)(2,1)}), bf16[4,536,3,192]{3,0,2,1:T(4,128)(2,1)}, u32[]{:S(2)}, u32[]{:S(2)}) async-start(bf16[4,536,3,192]{3,0,2,1:T(4,128)(2,1)} %copy.138), calls=%async_computation.3 | async-start | bytes 6586368 | tf_op jit(solution)/shard_map/all_to_all | solution.py:161
  314.8 181.3 %reduce-scatter.6.cloned.1.call-start = ((), (), s32[]{:S(2)}) async-start(), calls=%async_computation.8 | async-start | bytes 7299072 | tf_op jit(solution)/shard_map/reduce_scatter | solution.py:179
  373.9 263.9 %reduce-scatter.10.cloned.1.call-start = ((), (), s32[]{:S(2)}) async-start(), calls=%async_computation.10 | async-start | bytes 9732096 | tf_op jit(solution)/shard_map/reduce_scatter | solution.py:186
  384.1 395.2 %reduce-scatter.12.cloned.1.call-start = ((), (), s32[]{:S(2)}) async-start(), calls=%async_computation.11 | async-start | bytes 9732096 | tf_op jit(solution)/shard_map/reduce_scatter | solution.py:188
  395.9 12.5 %copy-start.11 = (f32[768]{0:T(1024)S(1)}, f32[768]{0:T(1024)}, u32[]{:S(2)}) copy-start(f32[768]{0:T(1024)} %param.26) | copy-start | bytes 9220
  395.9 12.5 %copy-start.14 = (f32[536]{0:T(1024)S(1)}, f32[536]{0:T(1024)}, u32[]{:S(2)}) copy-start(f32[536]{0:T(1024)} %copy-done.13) | copy-start | bytes 6436
  395.9 12.4 %copy-start.16 = (f32[536]{0:T(1024)S(1)}, f32[536]{0:T(1024)}, u32[]{:S(2)}) copy-start(f32[536]{0:T(1024)} %copy-done.15) | copy-start | bytes 6436
  408.3 5.6 copy-start.2
  408.3 5.6 copy-start.4
  418.8 7.6 copy-start.12
Sparse Core Ops, SparseCore 0:
  235.8 102.1 reduce-scatter.7
  374.0 122.0 reduce-scatter.5
  502.6 135.1 reduce-scatter.9
  644.1 135.1 reduce-scatter.11
where the time goes:
time: 795 us; the launch traced here: 786 us
  waiting for transfers between devices  407 us (51%)
  local copies, waits for them, and re-layouts  146 us (18%)
  matrix products  116 us (15%)
  blocking collectives  44.2 us (6%)
  other arithmetic  39.8 us (5%)
  starting transfers between devices  19 us (2%)
  between operations  14.3 us (2%)
    reduce_scatter x1, waiting for transfers between devices, local(): lax.psum_scatter(grad_up_weight, ('strip', 'seq'), scatter_dimension=0, t...  142 us
    reduce_scatter x1, waiting for transfers between devices, local(): lax.psum_scatter(grad_down_weight, ('strip', 'seq'), scatter_dimension=0,...  141 us
    all_to_all x1, waiting for transfers between devices, local(): lax.all_to_all(projected, 'seq', split_axis=3, concat_axis=1, tiled=True)  54.5 us
    unnamed x1, blocking collectives  44.2 us
    all_to_all x1, waiting for transfers between devices, local(): lax.all_to_all(grad_heads, 'seq', split_axis=1, concat_axis=3, tiled=True)  34.6 us
    dot_general x4, matrix products, weight_grad(): lax.dot_general(inputs, upstream, (((0,), (0,)), ((), ())), preferred_ele...  32.1 us
    unnamed x67, local copies, waits for them, and re-layouts  24 us
    dot_general x1, matrix products, local(): jnp.dot(inputs_two, up_weight, preferred_element_type=jnp.float32) + up_bias  20.2 us
  transfers between devices with their start and end apart: 8, of which 7 were waited for; matrix products, arithmetic and copies ran while one was open for 21% of the time, Pallas kernels for 0%

commit v1 on v0

--- a/solution.py
+++ b/solution.py
@@ -1,6 +1,10 @@
+import functools
+
 import jax
 import jax.numpy as jnp
 from jax import lax
+from jax.experimental import pallas as pl
+from jax.experimental.pallas import tpu as pltpu
 from jax.sharding import PartitionSpec as P
 
 HD = 64
@@ -92,7 +96,7 @@
     return stacked.reshape(block.shape).astype(jnp.bfloat16)
 
 
-def local(
+def local_general(
     patches,
     lengths,
     script,
@@ -208,6 +212,479 @@
     )
 
 
+MESH = pl.DeviceIdType.MESH
+BF = jnp.bfloat16
+F32 = jnp.float32
+CHUNKS = 24
+STAGES = 5
+WIDE = 384
+PART = 24
+
+
+def small_mesh(mesh):
+    return dict(mesh.shape) == {"strip": 8, "seq": 4}
+
+
+def dot(left, right, left_dim, right_dim):
+    return lax.dot_general(
+        left, right, (((left_dim,), (right_dim,)), ((), ())), preferred_element_type=F32
+    )
+
+
+def attend_forward_kernel(length_ref, q_ref, k_ref, v_ref, mixed_ref, lse_ref):
+    count = q_ref.shape[0]
+    lane = lax.broadcasted_iota(jnp.int32, (1, 128), 1)
+    visible = lax.broadcasted_iota(jnp.int32, (1, count), 1) < length_ref[0]
+    q = q_ref[...] * jnp.asarray(0.125, BF)
+    k = k_ref[...]
+    v = v_ref[...]
+    outs, logs = [], []
+    for head in range(2):
+        own = (lane // HD) == head
+        logits = dot(jnp.where(own, q, jnp.zeros_like(q)), k, 1, 1)
+        logits = jnp.where(visible, logits, -1000000000.0)
+        highest = jnp.max(logits, axis=1, keepdims=True)
+        expanded = jnp.exp(logits - highest)
+        total = jnp.sum(expanded, axis=1, keepdims=True)
+        probs = (expanded * (1.0 / total)).astype(BF)
+        outs.append(dot(probs, v, 1, 0))
+        logs.append(highest + jnp.log(total))
+    mixed_ref[...] = jnp.where(lane < HD, outs[0], outs[1]).astype(BF)
+    lse_ref[...] = jnp.where(lane < HD, logs[0], logs[1])
+
+
+def attend_backward_kernel(
+    length_ref, q_ref, k_ref, v_ref, gm_ref, lse_ref, gq_ref, gk_ref, gv_ref
+):
+    count = q_ref.shape[0]
+    lane = lax.broadcasted_iota(jnp.int32, (1, 128), 1)
+    visible = lax.broadcasted_iota(jnp.int32, (1, count), 1) < length_ref[0]
+    q = q_ref[...] * jnp.asarray(0.125, BF)
+    k = k_ref[...]
+    v = v_ref[...]
+    gm = gm_ref[...]
+    lse = lse_ref[...]
+    grads = []
+    for head in range(2):
+        own = (lane // HD) == head
+        q_own = jnp.where(own, q, jnp.zeros_like(q))
+        g_own = jnp.where(own, gm, jnp.zeros_like(gm))
+        k_own = jnp.where(own, k, jnp.zeros_like(k))
+        logits = dot(q_own, k, 1, 1)
+        probs = jnp.where(visible, jnp.exp(logits - lse[:, HD * head : HD * head + 1]), 0.0)
+        grad_probs = dot(g_own, v, 1, 1)
+        inner = jnp.sum(probs * grad_probs, axis=1, keepdims=True)
+        grad_logits = (probs * (grad_probs - inner)).astype(BF)
+        grads.append(
+            (
+                dot(grad_logits, k_own, 1, 0),
+                dot(q_own, grad_logits, 0, 0),
+                dot(g_own, probs.astype(BF), 0, 0),
+            )
+        )
+    gq_ref[...] = ((grads[0][0] + grads[1][0]) * 0.125).astype(BF)
+    gk_ref[...] = (grads[0][1] + grads[1][1]).T.astype(BF)
+    gv_ref[...] = (grads[0][2] + grads[1][2]).T.astype(BF)
+
+
+def head_block(count, offset):
+    return pl.BlockSpec((count, 128), lambda pair, *_: (0, pair + offset))
+
+
+def attend_forward_pairs(length, projected):
+    count, wide = projected.shape
+    pairs = wide // 384
+    return pl.pallas_call(
+        attend_forward_kernel,
+        grid_spec=pltpu.PrefetchScalarGridSpec(
+            num_scalar_prefetch=1,
+            grid=(pairs,),
+            in_specs=[head_block(count, pairs * part) for part in range(3)],
+            out_specs=[head_block(count, 0)] * 2,
+        ),
+        out_shape=[
+            jax.ShapeDtypeStruct((count, wide // 3), BF),
+            jax.ShapeDtypeStruct((count, wide // 3), F32),
+        ],
+    )(length, projected, projected, projected)
+
+
+def attend_backward_pairs(length, projected, grad_mixed, lse):
+    count, wide = projected.shape
+    pairs = wide // 384
+    return pl.pallas_call(
+        attend_backward_kernel,
+        grid_spec=pltpu.PrefetchScalarGridSpec(
+            num_scalar_prefetch=1,
+            grid=(pairs,),
+            in_specs=[head_block(count, pairs * part) for part in range(3)]
+            + [head_block(count, 0)] * 2,
+            out_specs=[head_block(count, 0)] * 3,
+        ),
+        out_shape=[jax.ShapeDtypeStruct((count, wide // 3), BF)] * 3,
+    )(length, projected, projected, projected, grad_mixed, lse)
+
+
+class Reduction:
+    def __init__(self, g, r1, r2, r3, r4, s4, r5, out, send, recv):
+        self.bufs = (g, r1, r2, r3, r4, s4, r5, out)
+        self.sems = (send, recv)
+        s, q = lax.axis_index("strip"), lax.axis_index("seq")
+        self.s, self.q = s, q
+        self.core, self.y = q % 2, q // 2
+        self.x, self.low, self.high = s % 2, (s // 2) % 2, s // 4
+        self.partners = [
+            (s, q + 1 - 2 * self.core),
+            (s, q + 2 - 4 * self.y),
+            (s + 1 - 2 * self.x, q),
+            (s + 2 - 4 * self.low, q),
+            (s + 4 - 8 * self.high, q),
+        ]
+
+    def side(self, c, second):
+        kind = (c + second) % 2
+        device = (
+            self.s + (1 - kind) * (1 - 2 * self.x),
+            self.q + kind * (2 - 4 * self.y),
+        )
+        return device, (1 - kind) * self.x + kind * self.y
+
+    def copy(self, stage, c):
+        g, r1, r2, r3, r4, s4, r5, _ = self.bufs
+        if stage == 0:
+            source, target, device = g.at[c, 1 - self.core], r1.at[c], self.partners[0]
+        elif stage == 1:
+            device, bit = self.side(c, 0)
+            source, target = r1.at[c, pl.ds((1 - bit) * 192, 192)], r2.at[c]
+        elif stage == 2:
+            device, bit = self.side(c, 1)
+            source, target = r2.at[c, pl.ds((1 - bit) * 96, 96)], r3.at[c]
+        elif stage == 3:
+            source, target = r3.at[c, pl.ds((1 - self.low) * 48, 48)], r4.at[c]
+            device = self.partners[3]
+        else:
+            source, target = s4.at[c, pl.ds((1 - self.high) * 24, 24)], r5.at[c]
+            device = self.partners[4]
+        send, recv = self.sems
+        return pltpu.make_async_remote_copy(
+            src_ref=source,
+            dst_ref=target,
+            send_sem=send.at[stage, c],
+            recv_sem=recv.at[stage, c],
+            device_id=device,
+            device_id_type=MESH,
+        )
+
+    def start(self, c):
+        self.copy(0, c).start()
+
+    def event(self, stage, c):
+        g, r1, r2, r3, r4, s4, r5, out = self.bufs
+        self.copy(stage, c).wait_recv()
+        if stage == 0:
+
+            @pl.loop(0, 4)
+            def _(i):
+                rows = pl.ds(i * 96, 96)
+                r1[c, rows] = r1[c, rows] + g[c, self.core, rows]
+        elif stage == 1:
+            _, bit = self.side(c, 0)
+
+            @pl.loop(0, 2)
+            def _(i):
+                kept = pl.ds(pl.multiple_of(bit * 192 + i * 96, 96), 96)
+                r2[c, pl.ds(i * 96, 96)] = r2[c, pl.ds(i * 96, 96)] + r1[c, kept]
+        elif stage == 2:
+            _, bit = self.side(c, 1)
+            r3[c] = r3[c] + r2[c, pl.ds(pl.multiple_of(bit * 96, 96), 96)]
+        elif stage == 3:
+            kept = pl.ds(pl.multiple_of(self.low * 48, 48), 48)
+            s4[c] = r4[c].astype(F32) + r3[c, kept].astype(F32)
+        else:
+            out[c] = s4[c, pl.ds(pl.multiple_of(self.high * 24, 24), 24)] + r5[c]
+            return
+        self.copy(stage + 1, c).start()
+
+    def tick(self, step, lags):
+        for stage, lag in enumerate(lags):
+            c = step - lag
+
+            @pl.when((c >= 0) & (c < CHUNKS))
+            def _():
+                self.event(stage, c)
+
+    def finish(self):
+        @pl.loop(0, CHUNKS)
+        def _(c):
+            for stage in range(STAGES):
+                self.copy(stage, c).wait_send()
+
+
+def reduce_vectors(red, vec, recvs, result, send, recv):
+    def copy(stage):
+        size = 64 >> stage
+        bit = (red.core, red.x, red.y, red.low, red.high)[stage]
+        device = [red.partners[i] for i in (0, 2, 1, 3, 4)][stage]
+        held = vec if stage == 0 else recvs[stage - 1]
+        return pltpu.make_async_remote_copy(
+            src_ref=held.at[pl.ds((1 - bit) * 2 * size, 2 * size)],
+            dst_ref=recvs[stage],
+            send_sem=send.at[stage],
+            recv_sem=recv.at[stage],
+            device_id=device,
+            device_id_type=MESH,
+        )
+
+    def event(stage):
+        size = 64 >> stage
+        bit = (red.core, red.x, red.y, red.low, red.high)[stage]
+        held = vec if stage == 0 else recvs[stage - 1]
+        copy(stage).wait_recv()
+        kept = held[pl.ds(pl.multiple_of(bit * 2 * size, 2 * size), 2 * size)]
+        if stage < STAGES - 1:
+            recvs[stage][...] = recvs[stage][...] + kept
+            copy(stage + 1).start()
+        else:
+            result[...] = recvs[stage][...] + kept
+
+    return copy, event
+
+
+def gradient_kernel(
+    n1, gq, gk, gv, mixed, branch, n2, gupper, active, cot, vec,
+    out, vec_out,
+    g, r1, r2, r3, r4, s4, r5, product, v1, v2, v3, v4, v5, send, recv, vsend, vrecv,
+):
+    red = Reduction(g, r1, r2, r3, r4, s4, r5, out, send, recv)
+    barrier = pltpu.get_barrier_semaphore()
+    for device in red.partners:
+        pl.semaphore_signal(barrier, inc=1, device_id=device, device_id_type=MESH)
+    pl.semaphore_wait(barrier, len(red.partners))
+    vec_copy, vec_event = reduce_vectors(red, vec, (v1, v2, v3, v4, v5), vec_out, vsend, vrecv)
+    vec_copy(0).start()
+    lags = (2, 4, 6, 8, 10)
+
+    def place(c, row_of):
+        kind = c % 2
+        for low_owner in range(16):
+            core, y, x, low = (
+                low_owner % 2, (low_owner // 2) % 2, (low_owner // 4) % 2, low_owner // 8,
+            )
+            unit = (1 - kind) * (4 * x + 2 * y + low) + kind * (4 * y + 2 * x + low)
+            if x == y:
+                unit = 4 * x + 2 * y + low
+            pair = jnp.concatenate(
+                [product[row_of(low_owner)], product[row_of(low_owner + 16)]], axis=0
+            )
+            where = unit * 48
+            if not isinstance(where, int):
+                where = pl.multiple_of(where, 48)
+            g[c, core, pl.ds(where, 48)] = pair.astype(BF)
+
+    plain = lambda owner: pl.ds(owner * PART, PART)
+
+    @pl.loop(0, 2)
+    def _(half):
+        columns = pl.ds(pl.multiple_of(half * WIDE, WIDE), WIDE)
+        right = cot[:, columns]
+        for block in range(4):
+            product[pl.ds(block * 768, 768)] = dot(
+                active[:, block * 768 : block * 768 + 768], right, 0, 0
+            )
+        for sub in range(4):
+            c = half * 4 + sub
+            place(c, lambda owner: pl.ds(owner * 96 + sub * PART, PART))
+            red.start(c)
+            red.tick(c, lags)
+
+    @pl.loop(8, 16)
+    def _(c):
+        columns = pl.ds(pl.multiple_of((c - 8) * WIDE, WIDE), WIDE)
+        product[pl.ds(0, 768)] = dot(n2[...], gupper[:, columns], 0, 0)
+        place(c, plain)
+        red.start(c)
+        red.tick(c, lags)
+
+    @pl.loop(16, 18)
+    def _(c):
+        columns = pl.ds(pl.multiple_of((c - 16) * WIDE, WIDE), WIDE)
+        product[pl.ds(0, 768)] = dot(mixed[...], branch[:, columns], 0, 0)
+        place(c, plain)
+        red.start(c)
+        red.tick(c, lags)
+
+    for part, grad in enumerate((gq, gk, gv)):
+
+        @pl.loop(18 + 2 * part, 20 + 2 * part)
+        def _(c):
+            columns = pl.ds(pl.multiple_of((c - 18 - 2 * part) * WIDE, WIDE), WIDE)
+            product[pl.ds(0, 768)] = dot(n1[...], grad[:, columns], 0, 0)
+            place(c, plain)
+            red.start(c)
+            red.tick(c, lags)
+
+    for stage in range(STAGES):
+        vec_event(stage)
+
+    @pl.loop(CHUNKS, CHUNKS + lags[-1])
+    def _(step):
+        red.tick(step, lags)
+
+    red.finish()
+    for stage in range(STAGES):
+        vec_copy(stage).wait_send()
+
+
+def reduce_gradients(*arrays):
+    rows = arrays[0].shape[0]
+    whole = pl.BlockSpec(memory_space=pltpu.VMEM)
+    return pl.pallas_call(
+        gradient_kernel,
+        out_shape=[
+            jax.ShapeDtypeStruct((CHUNKS, PART, WIDE), F32),
+            jax.ShapeDtypeStruct((8, 128), F32),
+        ],
+        in_specs=[whole] * len(arrays),
+        out_specs=[whole] * 2,
+        scratch_shapes=[
+            pltpu.VMEM((CHUNKS, 2, 384, WIDE), BF),
+            pltpu.VMEM((CHUNKS, 384, WIDE), BF),
+            pltpu.VMEM((CHUNKS, 192, WIDE), BF),
+            pltpu.VMEM((CHUNKS, 96, WIDE), BF),
+            pltpu.VMEM((CHUNKS, 48, WIDE), BF),
+            pltpu.VMEM((CHUNKS, 48, WIDE), F32),
+            pltpu.VMEM((CHUNKS, 24, WIDE), F32),
+            pltpu.VMEM((3072, WIDE), F32),
+        ]
+        + [pltpu.VMEM((128 >> stage, 128), F32) for stage in range(STAGES)]
+        + [
+            pltpu.SemaphoreType.DMA((STAGES, CHUNKS)),
+            pltpu.SemaphoreType.DMA((STAGES, CHUNKS)),
+            pltpu.SemaphoreType.DMA((STAGES,)),
+            pltpu.SemaphoreType.DMA((STAGES,)),
+        ],
+        compiler_params=pltpu.CompilerParams(
+            collective_id=0, has_side_effects=True, vmem_limit_bytes=60 << 20
+        ),
+    )(*arrays)
+
+
+def local(
+    patches,
+    lengths,
+    script,
+    script_table,
+    gain_one,
+    bias_one,
+    qkv_weight,
+    query_bias,
+    value_bias,
+    out_weight,
+    out_bias,
+    gain_two,
+    bias_two,
+    up_weight,
+    up_bias,
+    down_weight,
+    down_bias,
+    cotangent,
+):
+    strips, row_count, width = patches.shape
+    groups = script_table.shape[0]
+    tokens = strips * row_count
+    mine = lax.axis_index("seq")
+    length = lax.dynamic_slice(lengths, (mine,), (1,))
+    own_script = lax.dynamic_slice(script, (mine,), (1,))
+    selector = (own_script == jnp.arange(groups, dtype=jnp.int32)).astype(F32)
+    added = jnp.dot(selector.astype(BF), script_table, preferred_element_type=F32)
+    strip_in = lax.all_to_all(patches, "seq", 0, 0, tiled=True).reshape(tokens, width)
+    grad_result = lax.all_to_all(cotangent, "seq", 0, 0, tiled=True).reshape(tokens, width)
+    hidden = strip_in.astype(F32) + added[None, :]
+    normed_one, inverse_one = normalize(hidden)
+    inputs_one = (normed_one * gain_one + bias_one).astype(BF)
+    joint_bias = jnp.concatenate([query_bias, jnp.zeros_like(query_bias), value_bias])
+    projected = (
+        jnp.dot(inputs_one, qkv_weight, preferred_element_type=F32) + joint_bias
+    ).astype(BF)
+    mixed, lse = attend_forward_pairs(length, projected)
+    attended = hidden + jnp.dot(mixed, out_weight, preferred_element_type=F32) + out_bias
+    normed_two, inverse_two = normalize(attended)
+    inputs_two = (normed_two * gain_two + bias_two).astype(BF)
+    upper = jnp.dot(inputs_two, up_weight, preferred_element_type=F32) + up_bias
+    active = jax.nn.gelu(upper, approximate=False).astype(BF)
+    result = attended + jnp.dot(active, down_weight, preferred_element_type=F32) + down_bias
+    layer_out = lax.all_to_all(
+        result.astype(BF).reshape(strips, row_count, width), "seq", 0, 0, tiled=True
+    )
+    grad_float = grad_result.astype(F32)
+    grad_down_bias = jnp.sum(grad_float, axis=0)
+    grad_upper = (input_grad(grad_result, down_weight) * gelu_slope(upper)).astype(BF)
+    grad_up_bias = jnp.sum(grad_upper.astype(F32), axis=0)
+    grad_inputs_two = input_grad(grad_upper, up_weight)
+    grad_gain_two = jnp.sum(grad_inputs_two * normed_two, axis=0)
+    grad_bias_two = jnp.sum(grad_inputs_two, axis=0)
+    grad_attended = grad_float + norm_back(grad_inputs_two, gain_two, normed_two, inverse_two)
+    grad_branch = grad_attended.astype(BF)
+    grad_out_bias = jnp.sum(grad_branch.astype(F32), axis=0)
+    grad_mixed = input_grad(grad_branch, out_weight).astype(BF)
+    grad_q, grad_k, grad_v = attend_backward_pairs(length, projected, grad_mixed, lse)
+    grad_query_bias = jnp.sum(grad_q.astype(F32), axis=0)
+    grad_value_bias = jnp.sum(grad_v.astype(F32), axis=0)
+    grad_inputs_one = (
+        input_grad(grad_q, qkv_weight[:, :width])
+        + input_grad(grad_k, qkv_weight[:, width : 2 * width])
+        + input_grad(grad_v, qkv_weight[:, 2 * width :])
+    )
+    grad_gain_one = jnp.sum(grad_inputs_one * normed_one, axis=0)
+    grad_bias_one = jnp.sum(grad_inputs_one, axis=0)
+    grad_hidden = grad_attended + norm_back(grad_inputs_one, gain_one, normed_one, inverse_one)
+    grad_patches = lax.all_to_all(
+        grad_hidden.astype(BF).reshape(strips, row_count, width), "seq", 0, 0, tiled=True
+    )
+    grad_table = jnp.sum(grad_hidden, axis=0)[:, None] * selector[None, :]
+    owners = 32
+    small = [
+        grad_gain_one, grad_bias_one, grad_query_bias, grad_value_bias, grad_out_bias,
+        grad_gain_two, grad_bias_two, grad_down_bias, grad_up_bias, grad_table,
+    ]
+    packed = jnp.concatenate([v.reshape(owners, -1) for v in small], axis=1)
+    packed = jnp.pad(packed, ((0, 0), (0, 640))).reshape(2, 2, 2, 2, 2, 8, 128)
+    packed = packed.transpose(4, 2, 3, 1, 0, 5, 6).reshape(owners * 8, 128)
+    reduced, small_sum = reduce_gradients(
+        inputs_one, grad_q, grad_k, grad_v, mixed, grad_branch, inputs_two, grad_upper, active,
+        grad_result, packed,
+    )
+    flat = small_sum.reshape(-1)
+    part = width // owners
+    vectors = [flat[part * i : part * (i + 1)] for i in range(8)]
+    up_bias_sum = flat[8 * part : 12 * part]
+    table_sum = flat[12 * part : 16 * part].reshape(part, groups)
+    down_sum = (
+        reduced[0:8].reshape(2, 4, PART, WIDE).transpose(1, 2, 0, 3).reshape(4 * PART, width)
+    )
+    up_sum = reduced[8:16].transpose(1, 0, 2).reshape(PART, 8 * WIDE)
+    out_sum = reduced[16:18].transpose(1, 0, 2).reshape(PART, width)
+    qkv_sum = reduced[18:24].transpose(1, 0, 2).reshape(PART, 3 * width)
+    return (
+        layer_out,
+        grad_patches,
+        table_sum,
+        vectors[0],
+        vectors[1],
+        qkv_sum,
+        vectors[2],
+        vectors[3],
+        out_sum,
+        vectors[4],
+        vectors[5],
+        vectors[6],
+        up_sum,
+        up_bias_sum,
+        down_sum,
+        vectors[7],
+    )
+
+
 def solution(mesh):
     placed = (
         P("strip", "seq", None),
@@ -229,8 +706,9 @@
         P(),
         P("strip", "seq", None),
     )
+    chosen = local if small_mesh(mesh) else local_general
     return jax.shard_map(
-        local,
+        chosen,
         mesh=mesh,
         in_specs=placed,
         out_specs=(

time: 795 us -> 258 us (0.32); the launches traced: 786 us -> 257 us
  waiting for transfers between devices: 407 us -> 15.1 us
  Pallas kernels: 0 us -> 129 us
  local copies, waits for them, and re-layouts: 146 us -> 28 us
  matrix products: 116 us -> 59 us
  blocking collectives: 44.2 us -> 0 us
  other arithmetic: 39.8 us -> 8.62 us
  between operations: 14.3 us -> 1.22 us
    reduce_scatter x4 -> x0, waiting for transfers between devices: 291 us -> none  [the longest x1 142 us: local(): lax.psum_scatter(grad_up_weight, ('strip', 'seq'), scatter_dimension=0, t...]
    pallas_call x0 -> x3, Pallas kernels: none -> 129 us  [the longest x1 95.7 us: reduce_gradients(): pl.pallas_call(gradient_kernel, out_shape=[jax.ShapeDtypeStruct((CHUNKS,...]
    all_to_all x4, waiting for transfers between devices: 115 us -> 15.1 us  [the longest x1 8.39 us: local(): lax.all_to_all(patches, 'seq', 0, 0, tiled=True).reshape(tokens, width)]
    dot_general x38 -> x5, matrix products: 98.7 us -> 33.6 us  [the longest x1 19.1 us: local(): upper = jnp.dot(inputs_two, up_weight, preferred_element_type=F32) + up_bias]
    unnamed x1 -> x0, blocking collectives: 44.2 us -> none
    reshape x11 -> x15, local copies, waits for them, and re-layouts: 46 us -> 8.43 us  [the longest x1 2.28 us: local(): lax.all_to_all(cotangent, 'seq', 0, 0, tiled=True).reshape(tokens, width)]
    while x14 -> x0, local copies, waits for them, and re-layouts: 35.7 us -> none  [the longest x3 20.1 us: local(): mixed_heads, log_totals = lax.map(attend_forward, (head_blocks, lengths))]
    unnamed x67 -> x74, local copies, waits for them, and re-layouts: 24 us -> 12.8 us
  transfers between devices with their start and end apart: 8 -> 4, of which waited for: 7 -> 2; matrix products, arithmetic and copies ran while one was open for 21% -> 21% of each run, Pallas kernels for 0% -> 43%
where the time goes in v1:
time: 258 us; the launch traced here: 257 us
  Pallas kernels  129 us (50%)
  matrix products  59 us (23%)
  local copies, waits for them, and re-layouts  28 us (11%)
  starting transfers between devices  16.4 us (6%)
  waiting for transfers between devices  15.1 us (6%)
  other arithmetic  8.62 us (3%)
    pallas_call x1, Pallas kernels, reduce_gradients(): pl.pallas_call(gradient_kernel, out_shape=[jax.ShapeDtypeStruct((CHUNKS,...  95.7 us
    dot_general x6, matrix products, input_grad(): lax.dot_general(upstream, weight, (((1,), (1,)), ((), ())), preferred_ele...  25.4 us
    pallas_call x1, Pallas kernels, attend_backward_pairs(): pl.pallas_call(attend_backward_kernel, grid_spec=pltpu.PrefetchScalarGrid...  19.1 us
    dot_general x1, matrix products, local(): upper = jnp.dot(inputs_two, up_weight, preferred_element_type=F32) + up_bias  19.1 us
    pallas_call x1, Pallas kernels, attend_forward_pairs(): pl.pallas_call(attend_forward_kernel, grid_spec=pltpu.PrefetchScalarGridS...  13.9 us
    unnamed x74, local copies, waits for them, and re-layouts  12.8 us
    all_to_all x1, waiting for transfers between devices, local(): lax.all_to_all(patches, 'seq', 0, 0, tiled=True).reshape(tokens, width)  8.39 us
    all_to_all x1, waiting for transfers between devices, local(): lax.all_to_all(grad_hidden.astype(BF).reshape(strips, row_count, width),...  6.66 us
  transfers between devices with their start and end apart: 4, of which 2 were waited for; matrix products, arithmetic and copies ran while one was open for 21% of the time, Pallas kernels for 43%

profile of v1, /device:TPU:0, one launch (start us, length us, event | category | flops | bytes accessed | tf_op | source)
XLA Modules:
  0.0 257.2 jit_solution(7751168460332117245)
XLA Ops:
  0.7 2.3 copy.91
  3.0 4.3 %all-to-all-start = ((bf16[4,134,768]{2,1,0:T(8,128)(2,1)}), bf16[4,134,768]{2,1,0:T(8,128)(2,1)S(1)}, u32[]{:S(2)}, u32[]{:S(2)}) async-start(bf16[4,134,768]{2,1,0:T(8,128)(2,1)} %copy.91), calls=%async_computation | async-start | bytes 1671168 | tf_op jit(solution)/shard_map/all_to_all | solution.py:600
  7.3 0.6 dynamic_slice.6
  8.4 0.6 compare_convert_fusion
  9.2 1.0 copy.96
  10.2 0.8 convolution_reduce_fusion
  11.0 8.4 %all-to-all-done = bf16[4,134,768]{2,1,0:T(8,128)(2,1)S(1)} async-done(((bf16[4,134,768]{2,1,0:T(8,128)(2,1)}), bf16[4,134,768]{2,1,0:T(8,128)(2,1)S(1)}, u32[]{:S(2)}, u32[]{:S(2)}) %all-to-all-start) | async-done | bytes 823328 | tf_op jit(solution)/shard_map/all_to_all | solution.py:600
  19.4 4.2 %all-to-all-start.2 = ((bf16[4,134,768]{2,1,0:T(8,128)(2,1)}), bf16[4,134,768]{2,1,0:T(8,128)(2,1)}, u32[]{:S(2)}, u32[]{:S(2)}) async-start(bf16[4,134,768]{2,1,0:T(8,128)(2,1)} %copy.96), calls=%async_computation.2 | async-start | bytes 1671168 | tf_op jit(solution)/shard_map/all_to_all | solution.py:601
  24.5 1.3 reshape.206
  26.2 0.9 copy-done.8
  27.1 5.5 %add_convert_fusion.q_ref.k_ref.v_ref = bf16[536,2304]{1,0:T(8,128)(2,1)} fusion(bf16[536,768]{1,0:T(8,128)(2,1)S(1)} %add_convert_fusion.3.n1, bf16[768,2304]{1,0:T(8,128)(2,1)} %param.24, f32[2304]{0:T(1024)S(1)} %pad_maximum_fusion), kind=kOutput, calls=%fused_computation.27 | convolution fusion | flops 1899343872 | bytes 6841344 | tf_op jit(solution)/shard_map/dot_general | solution.py:607
  32.6 13.9 %shard_map.297 = (bf16[536,768]{1,0:T(8,128)(2,1)}, f32[536,768]{1,0:T(8,128)}) custom-call(s32[1]{0:T(128)} %dynamic_slice.7.length_ref, bf16[536,2304]{1,0:T(8,128)(2,1)} %add_convert_fusion.q_ref.k_ref.v_ref, bf16[536,2304]{1,0:T(8,128)(2,1)} %add_convert_fusion.q_ref.k_ref.v_ref, bf16[536,2304]{1,0:T(8,128)(2,1)} %add_convert_fusion.q_ref.k_ref.v_ref), custom_call_target="tpu_custom_call" | custom-call | tf_op jit(solution)/shard_map/pallas_call | solution.py:297
  46.6 2.2 fusion.24
  49.2 0.8 copy-done.1
  50.4 0.9 copy-done.9
  51.3 19.1 %fusion.2 = (bf16[536,3072]{1,0:T(8,128)(2,1)}, f32[536,3072]{1,0:T(8,128)}) fusion(f32[3072]{0:T(1024)S(1)} %copy-done.24, bf16[536,768]{1,0:T(8,128)(2,1)S(1)} %add_convert_fusion.2.n2, bf16[768,3072]{1,0:T(8,128)(2,1)S(1)} %bitcast.61), kind=kOutput, calls=%fused_computation.4 | convolution fusion | flops 2637840384 | bytes 15433728 | tf_op jit(solution)/shard_map/dot_general | solution.py:613
  70.3 2.3 reshape.187.cot
  72.6 7.9 %convert_reduce_fusion = (f32[3072]{0:T(1024)S(1)}, bf16[536,3072]{1,0:T(8,128)(2,1)S(1)}) fusion(f32[536,3072]{1,0:T(8,128)} %get-tuple-element.121, f32[3072]{0:T(1024)S(1)} %copy-done.24, bf16[536,768]{1,0:T(8,128)(2,1)} %reshape.187.cot, bf16[3072,768]{1,0:T(8,128)(2,1)} %param.33), kind=kOutput, calls=%fused_computation.11 | convolution fusion | flops 2550567936 | bytes 15446016 | tf_op jit(solution)/shard_map/dot_general | solution.py:38
  80.5 6.8 %multiply_reduce_fusion.1 = (f32[768]{0:T(1024)S(1)}, f32[536]{0:T(1024)S(1)}, f32[536]{0:T(1024)S(1)}, f32[768]{0:T(1024)S(1)}, f32[536,768]{1,0:T(8,128)S(1)}) fusion(f32[536,768]{1,0:T(8,128)S(1)} %copy-done.2, f32[536]{0:T(1024)S(1)} %add_rsqrt_fusion, f32[536]{0:T(1024)S(1)} %broadcast_multiply_fusion.5, f32[768]{0:T(1024)S(1)} %copy-done.18, ...), kind=kOutput, calls=%fused_computation.30 | convolution fusion | flops 2532867584 | bytes 11322752 | tf_op jit(solution)/shard_map/dot_general | solution.py:38
  87.3 1.9 convert_reduce_fusion.2
  89.2 0.9 copy-done.12
  90.2 1.7 convolution_convert_fusion.gm_ref
  91.9 19.1 %shard_map.298 = (bf16[536,768]{1,0:T(8,128)(2,1)}, bf16[536,768]{1,0:T(8,128)(2,1)}, bf16[536,768]{1,0:T(8,128)(2,1)}) custom-call(s32[1]{0:T(128)} %dynamic_slice.7.length_ref, bf16[536,2304]{1,0:T(8,128)(2,1)} %add_convert_fusion.q_ref.k_ref.v_ref, bf16[536,2304]{1,0:T(8,128)(2,1)} %add_convert_fusion.q_ref.k_ref.v_ref, ...), custom_call_target="tpu_custom_call" | custom-call | tf_op jit(solution)/shard_map/pallas_call | solution.py:315
  111.0 1.3 convert_reduce_fusion.4
  112.4 3.7 %fusion.19 = f32[536,768]{1,0:T(8,128)} fusion(bf16[536,768]{1,0:T(8,128)(2,1)} %get-tuple-element.25.gq, bf16[768,2304]{1,0:T(8,128)(2,1)} %param.24), kind=kOutput, calls=%fused_computation.54 | convolution fusion | flops 632291328 | bytes 3649536 | tf_op jit(solution)/shard_map/dot_general | solution.py:38
  116.1 6.0 %add_convert_fusion.1 = bf16[536,768]{1,0:T(8,128)(2,1)} fusion(f32[536,768]{1,0:T(8,128)S(1)} %copy-done.3, bf16[536,3072]{1,0:T(8,128)(2,1)S(1)} %copy-done.10, bf16[3072,768]{1,0:T(8,128)(2,1)} %param.33, f32[768]{0:T(1024)S(1)} %copy-done.27), kind=kOutput, calls=%fused_computation.40 | convolution fusion | flops 2530400256 | bytes 10484736 | tf_op jit(solution)/shard_map/dot_general | solution.py:615
  122.1 2.2 reshape.186
  124.3 4.4 %all-to-all-start.1 = ((bf16[4,134,768]{2,1,0:T(8,128)(2,1)}), bf16[4,134,768]{2,1,0:T(8,128)(2,1)}, u32[]{:S(2)}, u32[]{:S(2)}) async-start(bf16[4,134,768]{2,1,0:T(8,128)(2,1)} %reshape.186), calls=%async_computation.1 | async-start | bytes 1671168 | tf_op jit(solution)/shard_map/all_to_all | solution.py:616
  128.8 2.5 fusion.17
  131.4 2.8 %multiply_reduce_fusion.2 = (f32[768]{0:T(1024)S(1)}, f32[536]{0:T(1024)S(1)}, f32[536]{0:T(1024)S(1)}, f32[768]{0:T(1024)S(1)}, f32[536,768]{1,0:T(8,128)S(1)}) fusion(f32[536]{0:T(1024)S(1)} %rsqrt.20, f32[536]{0:T(1024)S(1)} %div.27, f32[536,768]{1,0:T(8,128)S(1)} %reshape.206, f32[768]{0:T(1024)S(1)} %convolution_reduce_fusion, f32[768]{0:T(1024)S(1)} %copy-done.17, ...), kind=kOutput, calls=%fused_computation.34 | convolution fusion | flops 637228544 | bytes 8610176 | tf_op jit(solution)/shard_map/dot_general | solution.py:38
  134.2 1.6 fusion.21
  135.8 1.3 convert_reduce_fusion.1
  138.4 0.7 copy.99
  139.1 95.7 %shard_map.299 = (f32[24,24,384]{2,1,0:T(8,128)}, f32[8,128]{1,0:T(8,128)}) custom-call(bf16[536,768]{1,0:T(8,128)(2,1)} %copy-done.8, bf16[536,768]{1,0:T(8,128)(2,1)} %get-tuple-element.25.gq, bf16[536,768]{1,0:T(8,128)(2,1)} %get-tuple-element.26.gk, bf16[536,768]{1,0:T(8,128)(2,1)} %get-tuple-element.27.gv, bf16[536,768]{1,0:T(8,128)(2,1)} %get-tuple-element.23.mixed, ...), custom_call_target="tpu_custom_call" | custom-call | tf_op jit(solution)/shard_map/pallas_call | solution.py:541
  234.9 0.9 slice.57
  235.7 1.3 slice.69
  237.0 0.9 slice_bitcast_fusion.2
  237.9 0.6 copy.110
  238.5 0.7 copy.106
  239.2 1.1 reshape.188
  240.3 3.5 %all-to-all-start.3 = ((bf16[4,134,768]{2,1,0:T(8,128)(2,1)}), bf16[4,134,768]{2,1,0:T(8,128)(2,1)S(1)}, u32[]{:S(2)}, u32[]{:S(2)}) async-start(bf16[4,134,768]{2,1,0:T(8,128)(2,1)} %reshape.188), calls=%async_computation.3 | async-start | bytes 1671168 | tf_op jit(solution)/shard_map/all_to_all | solution.py:641
  244.1 0.7 copy.113
  244.9 0.7 copy.109
  245.6 0.7 copy.111
  246.3 0.6 fusion.23
  246.9 2.4 copy.104
  249.3 6.7 %all-to-all-done.3 = bf16[4,134,768]{2,1,0:T(8,128)(2,1)S(1)} async-done(((bf16[4,134,768]{2,1,0:T(8,128)(2,1)}), bf16[4,134,768]{2,1,0:T(8,128)(2,1)S(1)}, u32[]{:S(2)}, u32[]{:S(2)}) %all-to-all-start.3) | async-done | bytes 823328 | tf_op jit(solution)/shard_map/all_to_all | solution.py:641
  255.9 1.2 copy.105
  (104 shorter events, 4.3 us)
Async XLA Ops:
  0.6 45.9 %copy-start = (bf16[768,768]{1,0:T(8,128)(2,1)S(1)}, bf16[768,768]{1,0:T(8,128)(2,1)}, u32[]{:S(2)}) copy-start(bf16[768,768]{1,0:T(8,128)(2,1)} %param.27) | copy-start | bytes 3538948
  0.7 6.6 %copy-start.28 = (s32[4]{0:T(128)S(1)}, s32[4]{0:T(128)}, u32[]{:S(2)}) copy-start(s32[4]{0:T(128)} %param.20) | copy-start | bytes 52
  0.7 7.2 %copy-start.29 = (s32[4]{0:T(128)S(1)}, s32[4]{0:T(128)}, u32[]{:S(2)}) copy-start(s32[4]{0:T(128)} %param.19) | copy-start | bytes 52
  0.7 8.5 %copy-start.16 = (bf16[4,134,768]{2,0,1:T(4,128)(2,1)S(1)}, bf16[4,134,768]{2,0,1:T(4,128)(2,1)}, u32[]{:S(2)}) copy-start(bf16[4,134,768]{2,0,1:T(4,128)(2,1)} %param.35) | copy-start | bytes 2469892
  0.7 9.5 %copy-start.22 = (f32[768]{0:T(1024)S(1)}, f32[768]{0:T(1024)}, u32[]{:S(2)}) copy-start(f32[768]{0:T(1024)} %param.26) | copy-start | bytes 9220
  0.7 9.5 %copy-start.23 = (f32[768]{0:T(1024)S(1)}, f32[768]{0:T(1024)}, u32[]{:S(2)}) copy-start(f32[768]{0:T(1024)} %param.25) | copy-start | bytes 9220
  0.7 9.5 %copy-start.25 = (bf16[4,768]{1,0:T(4,128)(2,1)S(1)}, bf16[4,768]{1,0:T(4,128)(2,1)}, u32[]{:S(2)}) copy-start(bf16[4,768]{1,0:T(4,128)(2,1)} %param.21) | copy-start | bytes 18436
  3.0 16.4 %all-to-all-start = ((bf16[4,134,768]{2,1,0:T(8,128)(2,1)}), bf16[4,134,768]{2,1,0:T(8,128)(2,1)S(1)}, u32[]{:S(2)}, u32[]{:S(2)}) async-start(bf16[4,134,768]{2,1,0:T(8,128)(2,1)} %copy.91), calls=%async_computation | async-start | bytes 1671168 | tf_op jit(solution)/shard_map/all_to_all | solution.py:600
  10.2 15.6 %copy-start.17 = (f32[768]{0:T(1024)S(1)}, f32[768]{0:T(1024)}, u32[]{:S(2)}) copy-start(f32[768]{0:T(1024)} %param.22) | copy-start | bytes 9220
  10.2 15.6 %copy-start.20 = (f32[768]{0:T(1024)S(1)}, f32[768]{0:T(1024)}, u32[]{:S(2)}) copy-start(f32[768]{0:T(1024)} %param.23) | copy-start | bytes 9220
  19.4 5.0 %copy-start.4 = (bf16[4,134,768]{2,1,0:T(8,128)(2,1)}, bf16[4,134,768]{2,1,0:T(8,128)(2,1)S(1)}, u32[]{:S(2)}) copy-start(bf16[4,134,768]{2,1,0:T(8,128)(2,1)S(1)} %all-to-all-done) | copy-start | bytes 2469892
  19.4 50.9 %all-to-all-start.2 = ((bf16[4,134,768]{2,1,0:T(8,128)(2,1)}), bf16[4,134,768]{2,1,0:T(8,128)(2,1)}, u32[]{:S(2)}, u32[]{:S(2)}) async-start(bf16[4,134,768]{2,1,0:T(8,128)(2,1)} %copy.96), calls=%async_computation.2 | async-start | bytes 1671168 | tf_op jit(solution)/shard_map/all_to_all | solution.py:601
  26.2 0.9 copy-start.8
  32.6 13.9 %copy-start.26 = (f32[768]{0:T(1024)S(1)}, f32[768]{0:T(1024)}, u32[]{:S(2)}) copy-start(f32[768]{0:T(1024)} %param.28) | copy-start | bytes 9220
  46.5 4.7 %slice-start = ((s8[4718592]{0:T(1024)(128)(4,1)}), s8[4194304]{0:T(1024)(128)(4,1)S(1)}, s32[]{:S(2)}) async-start(s8[4718592]{0:T(1024)(128)(4,1)} %bitcast.60), calls=%async_computation.4 | async-start | bytes 8388608
  46.6 3.5 %copy-start.18 = (f32[768]{0:T(1024)S(1)}, f32[768]{0:T(1024)}, u32[]{:S(2)}) copy-start(f32[768]{0:T(1024)} %param.29) | copy-start | bytes 9220
  46.6 3.5 %copy-start.21 = (f32[768]{0:T(1024)S(1)}, f32[768]{0:T(1024)}, u32[]{:S(2)}) copy-start(f32[768]{0:T(1024)} %param.30) | copy-start | bytes 9220
  46.6 4.7 %slice-start.1 = ((s8[4718592]{0:T(1024)(128)(4,1)}), s8[524288]{0:T(1024)(128)(4,1)S(1)}, s32[]{:S(2)}) async-start(s8[4718592]{0:T(1024)(128)(4,1)} %bitcast.60), calls=%async_computation.5 | async-start | bytes 1048576
  48.8 1.2 copy-start.1
  48.9 2.4 copy-start.24
  50.4 0.9 copy-start.9
  72.6 7.9 %copy-start.2 = (f32[536,768]{1,0:T(8,128)S(1)}, f32[536,768]{1,0:T(8,128)}, u32[]{:S(2)}) copy-start(f32[536,768]{1,0:T(8,128)} %copy-done.1) | copy-start | bytes 4939780
  80.5 6.8 %copy-start.11 = (bf16[536,3072]{1,0:T(8,128)(2,1)}, bf16[536,3072]{1,0:T(8,128)(2,1)S(1)}, u32[]{:S(2)}) copy-start(bf16[536,3072]{1,0:T(8,128)(2,1)S(1)} %get-tuple-element.124.gupper) | copy-start | bytes 9879556
  80.5 6.8 %copy-start.6 = (bf16[536,768]{1,0:T(8,128)(2,1)S(1)}, bf16[536,768]{1,0:T(8,128)(2,1)}, u32[]{:S(2)}) copy-start(bf16[536,768]{1,0:T(8,128)(2,1)} %reshape.187.cot) | copy-start | bytes 2469892
  89.2 0.9 copy-start.12
  112.3 3.7 %copy-start.3 = (f32[536,768]{1,0:T(8,128)S(1)}, f32[536,768]{1,0:T(8,128)}, u32[]{:S(2)}) copy-start(f32[536,768]{1,0:T(8,128)} %copy-done.1) | copy-start | bytes 4939780
  112.3 3.7 %copy-start.10 = (bf16[536,3072]{1,0:T(8,128)(2,1)S(1)}, bf16[536,3072]{1,0:T(8,128)(2,1)}, u32[]{:S(2)}) copy-start(bf16[536,3072]{1,0:T(8,128)(2,1)} %get-tuple-element.120.active) | copy-start | bytes 9879556
  112.3 3.7 %copy-start.27 = (f32[768]{0:T(1024)S(1)}, f32[768]{0:T(1024)}, u32[]{:S(2)}) copy-start(f32[768]{0:T(1024)} %param.34) | copy-start | bytes 9220
  124.3 116.0 %all-to-all-start.1 = ((bf16[4,134,768]{2,1,0:T(8,128)(2,1)}), bf16[4,134,768]{2,1,0:T(8,128)(2,1)}, u32[]{:S(2)}, u32[]{:S(2)}) async-start(bf16[4,134,768]{2,1,0:T(8,128)(2,1)} %reshape.186), calls=%async_computation.1 | async-start | bytes 1671168 | tf_op jit(solution)/shard_map/all_to_all | solution.py:616
  128.8 2.6 copy-start.5
  128.8 2.6 copy-start.14
  131.4 2.9 %copy-start.7 = (f32[536,768]{1,0:T(8,128)S(1)}, f32[536,768]{1,0:T(8,128)}, u32[]{:S(2)}) copy-start(f32[536,768]{1,0:T(8,128)} %get-tuple-element.106) | copy-start | bytes 4939780
  139.1 100.1 %copy-start.13 = (bf16[536,768]{1,0:T(8,128)(2,1)S(1)}, bf16[536,768]{1,0:T(8,128)(2,1)}, u32[]{:S(2)}) copy-start(bf16[536,768]{1,0:T(8,128)(2,1)} %get-tuple-element.103) | copy-start | bytes 2469892
  234.8 9.0 %copy-start.15 = (f32[24,24,384]{2,1,0:T(8,128)S(1)}, f32[24,24,384]{2,1,0:T(8,128)}, u32[]{:S(2)}) copy-start(f32[24,24,384]{2,1,0:T(8,128)} %get-tuple-element.29) | copy-start | bytes 2654212
  239.2 7.1 %copy-start.19 = (f32[8,128]{1,0:T(8,128)S(1)}, f32[8,128]{1,0:T(8,128)}, u32[]{:S(2)}) copy-start(f32[8,128]{1,0:T(8,128)} %get-tuple-element.28) | copy-start | bytes 12292
  240.3 15.6 %all-to-all-start.3 = ((bf16[4,134,768]{2,1,0:T(8,128)(2,1)}), bf16[4,134,768]{2,1,0:T(8,128)(2,1)S(1)}, u32[]{:S(2)}, u32[]{:S(2)}) async-start(bf16[4,134,768]{2,1,0:T(8,128)(2,1)} %reshape.188), calls=%async_computation.3 | async-start | bytes 1671168 | tf_op jit(solution)/shard_map/all_to_all | solution.py:641

commit v2 on v0

--- a/solution.py
+++ b/solution.py
@@ -1,6 +1,10 @@
+import functools
+
 import jax
 import jax.numpy as jnp
 from jax import lax
+from jax.experimental import pallas as pl
+from jax.experimental.pallas import tpu as pltpu
 from jax.sharding import PartitionSpec as P
 
 HD = 64
@@ -92,7 +96,7 @@
     return stacked.reshape(block.shape).astype(jnp.bfloat16)
 
 
-def local(
+def local_general(
     patches,
     lengths,
     script,
@@ -208,6 +212,761 @@
     )
 
 
+MESH = pl.DeviceIdType.MESH
+BF = jnp.bfloat16
+F32 = jnp.float32
+CHUNKS = 24
+SLOTS = 12
+STAGES = 5
+WIDE = 384
+PART = 24
+BLOCK = 32
+LAGS = (2, 5, 7, 9, 11)
+
+
+def fits(mesh):
+    return dict(mesh.shape) == {"strip": 8, "seq": 4}
+
+
+def dot(left, right, left_dim, right_dim):
+    return lax.dot_general(
+        left, right, (((left_dim,), (right_dim,)), ((), ())), preferred_element_type=F32
+    )
+
+
+def mean(block):
+    return jnp.mean(block, axis=1, keepdims=True)
+
+
+def fold(block):
+    return jnp.sum(block.reshape(block.shape[0] // 8, 8, block.shape[1]), axis=0)
+
+
+def column_sum(block):
+    return jnp.sum(block, axis=0, keepdims=True)
+
+
+def attend_pair(pair, length, proj, mixed, lse_all):
+    count = proj.shape[0]
+    width = proj.shape[1] // 3
+    at = lambda part: pl.ds(pl.multiple_of(part * width + pair * 128, 128), 128)
+    lane = lax.broadcasted_iota(jnp.int32, (1, 128), 1)
+    visible = lax.broadcasted_iota(jnp.int32, (1, count), 1) < length
+    q = proj[:, at(0)] * jnp.asarray(0.125, BF)
+    k = proj[:, at(1)]
+    v = proj[:, at(2)]
+    outs, logs = [], []
+    for head in range(2):
+        own = (lane // HD) == head
+        logits = dot(jnp.where(own, q, jnp.zeros_like(q)), k, 1, 1)
+        logits = jnp.where(visible, logits, -1000000000.0)
+        highest = jnp.max(logits, axis=1, keepdims=True)
+        expanded = jnp.exp(logits - highest)
+        total = jnp.sum(expanded, axis=1, keepdims=True)
+        probs = (expanded * (1.0 / total)).astype(BF)
+        outs.append(dot(probs, v, 1, 0))
+        logs.append(highest + jnp.log(total))
+    mixed[:, at(0)] = jnp.where(lane < HD, outs[0], outs[1]).astype(BF)
+    known = jnp.where(lane == 2 * pair, logs[0], lse_all[...])
+    lse_all[...] = jnp.where(lane == 2 * pair + 1, logs[1], known)
+
+
+def attend_pair_back(pair, length, proj, gmixed, lse_all):
+    count = proj.shape[0]
+    width = proj.shape[1] // 3
+    at = lambda part: pl.ds(pl.multiple_of(part * width + pair * 128, 128), 128)
+    lane = lax.broadcasted_iota(jnp.int32, (1, 128), 1)
+    visible = lax.broadcasted_iota(jnp.int32, (1, count), 1) < length
+    q = proj[:, at(0)] * jnp.asarray(0.125, BF)
+    k = proj[:, at(1)]
+    v = proj[:, at(2)]
+    gm = gmixed[:, at(0)]
+    lse = lse_all[...]
+    grads = []
+    for head in range(2):
+        own = (lane // HD) == head
+        q_own = jnp.where(own, q, jnp.zeros_like(q))
+        g_own = jnp.where(own, gm, jnp.zeros_like(gm))
+        k_own = jnp.where(own, k, jnp.zeros_like(k))
+        own_lse = jnp.sum(jnp.where(lane == 2 * pair + head, lse, 0.0), axis=1, keepdims=True)
+        logits = dot(q_own, k, 1, 1)
+        probs = jnp.where(visible, jnp.exp(logits - own_lse), 0.0)
+        grad_probs = dot(g_own, v, 1, 1)
+        inner = jnp.sum(probs * grad_probs, axis=1, keepdims=True)
+        grad_logits = (probs * (grad_probs - inner)).astype(BF)
+        grads.append(
+            (
+                dot(grad_logits, k_own, 1, 0),
+                dot(q_own, grad_logits, 0, 0),
+                dot(g_own, probs.astype(BF), 0, 0),
+            )
+        )
+    gq = ((grads[0][0] + grads[1][0]) * 0.125).astype(BF)
+    gk = (grads[0][1] + grads[1][1]).T.astype(BF)
+    gv = (grads[0][2] + grads[1][2]).T.astype(BF)
+    return gq, gk, gv
+
+
+class Devices:
+    def __init__(self):
+        s, q = lax.axis_index("strip"), lax.axis_index("seq")
+        self.s, self.q = s, q
+        self.core, self.y = q % 2, q // 2
+        self.x, self.low, self.high = s % 2, (s // 2) % 2, s // 4
+        self.to_core = (s, q + 1 - 2 * self.core)
+        self.to_y = (s, q + 2 - 4 * self.y)
+        self.to_x = (s + 1 - 2 * self.x, q)
+        self.to_low = (s + 2 - 4 * self.low, q)
+        self.to_high = (s + 4 - 8 * self.high, q)
+
+
+def kinds(c):
+    kind = c % 3
+    return (2 - kind) * (1 - kind) // 2, kind * (2 - kind), kind * (kind - 1) // 2
+
+
+class Reduction:
+    def __init__(self, dev, g, r1, r2, r3, r4, s4, r5, write, send, recv):
+        self.dev = dev
+        self.bufs = (g, r1, r2, r3, r4, s4, r5)
+        self.write = write
+        self.sems = (send, recv)
+
+    def side(self, stage, c):
+        dev = self.dev
+        in_x, in_y, in_z = kinds(c)
+        if stage == 1:
+            by_x, by_y, by_low = in_x, in_y, in_z
+        elif stage == 2:
+            by_x, by_y, by_low = in_y + in_z, in_x, 0
+        else:
+            by_x, by_y, by_low = 0, in_z, in_x + in_y
+        device = (
+            dev.s + by_x * (1 - 2 * dev.x) + by_low * (2 - 4 * dev.low),
+            dev.q + by_y * (2 - 4 * dev.y),
+        )
+        return device, by_x * dev.x + by_y * dev.y + by_low * dev.low
+
+    def copy(self, stage, c):
+        g, r1, r2, r3, r4, s4, r5 = self.bufs
+        dev = self.dev
+        if stage == 0:
+            source, target, device = g.at[c % SLOTS, 1 - dev.core], r1.at[c], dev.to_core
+        elif stage == 4:
+            source, target = s4.at[c, pl.ds((1 - dev.high) * 24, 24)], r5.at[c]
+            device = dev.to_high
+        else:
+            device, bit = self.side(stage, c)
+            rows = 384 >> stage
+            held, target = ((r1, r2), (r2, r3), (r3, r4))[stage - 1]
+            source, target = held.at[c, pl.ds((1 - bit) * rows, rows)], target.at[c]
+        send, recv = self.sems
+        return pltpu.make_async_remote_copy(
+            src_ref=source,
+            dst_ref=target,
+            send_sem=send.at[stage, c],
+            recv_sem=recv.at[stage, c],
+            device_id=device,
+            device_id_type=MESH,
+        )
+
+    def free(self, c):
+        @pl.when(c >= SLOTS)
+        def _():
+            self.copy(0, c - SLOTS).wait_send()
+
+    def start(self, c):
+        self.copy(0, c).start()
+
+    def event(self, stage, c):
+        g, r1, r2, r3, r4, s4, r5 = self.bufs
+        dev = self.dev
+        self.copy(stage, c).wait_recv()
+        if stage == 0:
+
+            @pl.loop(0, 4)
+            def _(i):
+                rows = pl.ds(i * 96, 96)
+                r1[c, rows] = r1[c, rows] + g[c % SLOTS, dev.core, rows]
+        elif stage < 3:
+            _, bit = self.side(stage, c)
+            held, target = ((r1, r2), (r2, r3))[stage - 1]
+
+            @pl.loop(0, 4 >> stage)
+            def _(i):
+                rows = pl.ds(i * 96, 96)
+                kept = pl.ds(pl.multiple_of(bit * (384 >> stage) + i * 96, 96), 96)
+                target[c, rows] = target[c, rows] + held[c, kept]
+        elif stage == 3:
+            _, bit = self.side(stage, c)
+            kept = pl.ds(pl.multiple_of(bit * 48, 48), 48)
+            s4[c] = r4[c].astype(F32) + r3[c, kept].astype(F32)
+        else:
+            self.write[c] = s4[c, pl.ds(pl.multiple_of(dev.high * 24, 24), 24)] + r5[c]
+            return
+        self.copy(stage + 1, c).start()
+
+    def tick(self, step):
+        for stage, lag in enumerate(LAGS):
+            c = step - lag
+
+            @pl.when((c >= 0) & (c < CHUNKS))
+            def _():
+                self.event(stage, c)
+
+    def finish(self):
+        @pl.loop(0, CHUNKS)
+        def _(c):
+            for stage in range(1, STAGES):
+                self.copy(stage, c).wait_send()
+
+        @pl.loop(CHUNKS - SLOTS, CHUNKS)
+        def _(c):
+            self.copy(0, c).wait_send()
+
+    def put(self, c, core, x, y, low, rows):
+        in_x, in_y, in_z = kinds(c)
+        unit = (
+            in_x * (4 * x + 2 * y + low)
+            + in_y * (4 * y + 2 * x + low)
+            + in_z * (4 * low + 2 * x + y)
+        )
+        where = unit * 48
+        if not isinstance(where, int):
+            where = pl.multiple_of(where, 48)
+        self.bufs[0][c % SLOTS, core, pl.ds(where, 48)] = rows.astype(BF)
+
+    def place(self, c, half, product):
+        columns = pl.ds(half * WIDE, WIDE)
+        for owner in range(16):
+            pair = jnp.concatenate(
+                [
+                    product[pl.ds(owner * PART, PART), columns],
+                    product[pl.ds((owner + 16) * PART, PART), columns],
+                ],
+                axis=0,
+            )
+            self.put(c, owner % 2, (owner // 4) % 2, (owner // 2) % 2, owner // 8, pair)
+
+
+ERF_TOP = (
+    0.00022905065861350646, 0.0034082910107109506, 0.050955695062380861, 0.18520832239976145,
+    1.128379143519084,
+)
+ERF_BOTTOM = (
+    -1.1791602954361697e-7, 0.000023547966471313185, 0.0010179625278914885,
+    0.014070470171167667, 0.11098505178285362, 0.49746925110067538, 1.0,
+)
+
+
+def erf(value):
+    value = jnp.clip(value, -3.832506856900711, 3.832506856900711)
+    square = value * value
+    top = jnp.full_like(square, ERF_TOP[0])
+    for term in ERF_TOP[1:]:
+        top = top * square + term
+    bottom = jnp.full_like(square, ERF_BOTTOM[0])
+    for term in ERF_BOTTOM[1:]:
+        bottom = bottom * square + term
+    return value * top / bottom
+
+
+def standardize(block):
+    centred = block - mean(block)
+    inverse = lax.rsqrt(mean(centred * centred) + epsilon)
+    return centred * inverse, inverse
+
+
+def layer_kernel(
+    lengths, script, table, gain_one, bias_one, query_bias, value_bias, out_bias, gain_two,
+    bias_two, up_bias, down_bias, patches, cotangent, qkv_hbm, out_hbm, up_hbm, down_hbm,
+    layer_out, grad_patches, reduced, small,
+    xin, cin, hidden, n1, proj, mixed, lse_all, att, n2, active, cot, res, gn, branch, gmixed,
+    gblk, product, jbias, vecs, wqkv, wout, wup, wdown,
+    g, r1, r2, r3, r4, s4, r5, v1, v2, v3, v4, v5,
+    send, recv, vsend, vrecv, xsend, xrecv, wsem, fsem, osem,
+):
+    strips, row_count, width = patches.shape
+    count = strips * row_count
+    rows = hidden.shape[0]
+    blocks = rows // BLOCK
+    ff_blocks = up_hbm.shape[1] // width
+    dev = Devices()
+    s, q = dev.s, dev.q
+    red = Reduction(dev, g, r1, r2, r3, r4, s4, r5, reduced, send, recv)
+
+    barrier = pltpu.get_barrier_semaphore()
+    greeted = [(s, (q + hop) % strips) for hop in range(1, strips)]
+    greeted += [dev.to_x, dev.to_low, dev.to_high]
+    for device in greeted:
+        pl.semaphore_signal(barrier, inc=1, device_id=device, device_id_type=MESH)
+
+    load_qkv = pltpu.make_async_copy(qkv_hbm, wqkv, wsem.at[0])
+    load_out = pltpu.make_async_copy(out_hbm, wout, wsem.at[1])
+
+    def load_ff(block):
+        columns = pl.ds(pl.multiple_of(block * width, width), width)
+        slot = block % 2
+        return (
+            pltpu.make_async_copy(up_hbm.at[:, columns], wup.at[slot], fsem.at[0, slot]),
+            pltpu.make_async_copy(down_hbm.at[columns], wdown.at[slot], fsem.at[1, slot]),
+        )
+
+    def exchange(group, source, target):
+        copies = []
+        for hop in range(1, strips):
+            other = (q + hop) % strips
+            copies.append(
+                pltpu.make_async_remote_copy(
+                    src_ref=source.at[other],
+                    dst_ref=target.at[q],
+                    send_sem=xsend.at[group, hop],
+                    recv_sem=xrecv.at[group, hop],
+                    device_id=(s, other),
+                    device_id_type=MESH,
+                )
+            )
+        own = pltpu.make_async_copy(source.at[q], target.at[q], osem.at[group])
+        return copies, own
+
+    def launch(moves):
+        copies, own = moves
+        for index in (1, 0, 2):
+            copies[index].start()
+        own.start()
+
+    def arrive(moves):
+        copies, own = moves
+        for copy in copies:
+            copy.wait_recv()
+        own.wait()
+
+    into_x = exchange(0, patches, xin)
+    into_c = exchange(1, cotangent, cin)
+    pl.semaphore_wait(barrier, len(greeted))
+    launch(into_x)
+    load_qkv.start()
+    load_out.start()
+    for copy in load_ff(0):
+        copy.start()
+    launch(into_c)
+
+    length = lengths[q]
+    own_script = script[q]
+    added = jnp.zeros((1, width), F32)
+    for group in range(table.shape[0]):
+        added = jnp.where(own_script == group, table[pl.ds(group, 1)].astype(F32), added)
+    row = lambda ref: ref[...].reshape(1, ref.shape[0])
+    jbias[pl.ds(0, 1)] = row(query_bias)
+    jbias[pl.ds(1, 1)] = jnp.zeros((1, width), F32)
+    jbias[pl.ds(2, 1)] = row(value_bias)
+    hidden[pl.ds(count, rows - count)] = jnp.zeros((rows - count, width), F32)
+    gn[pl.ds(count, rows - count)] = jnp.zeros((rows - count, width), F32)
+    lse_all[...] = jnp.zeros_like(lse_all)
+
+    arrive(into_x)
+    for j in range(strips):
+        hidden[pl.ds(j * row_count, row_count)] = xin[j].astype(F32) + added
+
+    @pl.loop(0, blocks)
+    def _(b):
+        at = pl.ds(pl.multiple_of(b * BLOCK, BLOCK), BLOCK)
+        normed, _ = standardize(hidden[at])
+        n1[at] = (normed * row(gain_one) + row(bias_one)).astype(BF)
+
+    load_qkv.wait()
+
+    @pl.loop(0, 3)
+    def _(part):
+        columns = pl.ds(pl.multiple_of(part * width, width), width)
+        proj[:, columns] = (dot(n1[...], wqkv[:, columns], 1, 0) + jbias[pl.ds(part, 1)]).astype(BF)
+
+    @pl.loop(0, width // 128)
+    def _(pair):
+        attend_pair(pair, length, proj, mixed, lse_all)
+
+    arrive(into_c)
+    for j in range(strips):
+        gn[pl.ds(j * row_count, row_count)] = cin[j].astype(F32)
+    load_out.wait()
+    att[...] = hidden[...] + dot(mixed[...], wout[...], 1, 0) + row(out_bias)
+    zero8 = jnp.zeros((8, width), F32)
+
+    def second_norm(b, total):
+        at = pl.ds(pl.multiple_of(b * BLOCK, BLOCK), BLOCK)
+        block = att[at]
+        normed, _ = standardize(block)
+        n2[at] = (normed * row(gain_two) + row(bias_two)).astype(BF)
+        res[at] = block + row(down_bias)
+        upstream = gn[at]
+        cot[at] = upstream.astype(BF)
+        gn[at] = jnp.zeros((BLOCK, width), F32)
+        return total + fold(upstream)
+
+    vecs[pl.ds(7, 1)] = column_sum(lax.fori_loop(0, blocks, second_norm, zero8))
+
+    @pl.loop(0, ff_blocks)
+    def _(block):
+        slot = block % 2
+        for copy in load_ff(block):
+            copy.wait()
+
+        @pl.when(block + 1 < ff_blocks)
+        def _():
+            for copy in load_ff(block + 1):
+                copy.start()
+
+        up = wup[slot]
+        down = wdown[slot]
+        upper = dot(n2[...], up, 1, 0) + up_bias[pl.ds(block, 1)]
+        grad_active = dot(cot[...], down, 1, 1)
+        share = 0.5 * (1.0 + erf(upper * 0.7071067811865476))
+        columns = pl.ds(pl.multiple_of(block * width, width), width)
+        act = (upper * share).astype(BF)
+        active[:, columns] = act
+        slope = share + upper * jnp.exp(-0.5 * upper * upper) * 0.3989422804014327
+        grad_upper = (grad_active * slope).astype(BF)
+        gblk[...] = grad_upper
+        res[...] += dot(act, down, 1, 0)
+        gn[...] += dot(grad_upper, up, 1, 1)
+        vecs[pl.ds(12 + block, 1)] = column_sum(grad_upper.astype(F32))
+        product[...] = dot(n2[...], gblk[...], 0, 0)
+        for half in range(2):
+            c = 2 * block + half
+            red.free(c)
+            red.place(c, half, product)
+            red.start(c)
+            red.tick(c)
+
+    for j in range(strips):
+        xin[j] = res[pl.ds(j * row_count, row_count)].astype(BF)
+    from_out = exchange(2, xin, layer_out)
+    launch(from_out)
+
+    def second_back(b, totals):
+        at = pl.ds(pl.multiple_of(b * BLOCK, BLOCK), BLOCK)
+        normed, inverse = standardize(att[at])
+        upstream = gn[at]
+        scaled = upstream * row(gain_two)
+        back = inverse * (scaled - mean(scaled) - normed * mean(scaled * normed))
+        grad = cot[at].astype(F32) + back
+        rounded = grad.astype(BF)
+        gn[at] = grad
+        branch[at] = rounded
+        return (
+            totals[0] + fold(upstream * normed),
+            totals[1] + fold(upstream),
+            totals[2] + fold(rounded.astype(F32)),
+        )
+
+    totals = lax.fori_loop(0, blocks, second_back, (zero8, zero8, zero8))
+    vecs[pl.ds(5, 1)] = column_sum(totals[0])
+    vecs[pl.ds(6, 1)] = column_sum(totals[1])
+    vecs[pl.ds(4, 1)] = column_sum(totals[2])
+    gmixed[...] = dot(branch[...], wout[...], 1, 1).astype(BF)
+    product[...] = dot(mixed[...], branch[...], 0, 0)
+    for half in range(2):
+        c = 8 + half
+        red.free(c)
+        red.place(c, half, product)
+        red.start(c)
+        red.tick(c)
+
+    @pl.loop(10, 18)
+    def _(c):
+        red.free(c)
+
+    @pl.loop(0, 4)
+    def _(b):
+        left = jnp.concatenate(
+            [
+                active[:, pl.ds(pl.multiple_of(b * WIDE, WIDE), WIDE)],
+                active[:, pl.ds(pl.multiple_of(4 * WIDE + b * WIDE, WIDE), WIDE)],
+            ],
+            axis=1,
+        )
+        product[...] = dot(left, cot[...], 0, 0)
+        for half in range(2):
+            for sub in range(4):
+                for near in range(4):
+                    at = near * 4 * PART + sub * PART
+                    columns = pl.ds(half * WIDE, WIDE)
+                    pair = jnp.concatenate(
+                        [
+                            product[pl.ds(at, PART), columns],
+                            product[pl.ds(at + 384, PART), columns],
+                        ],
+                        axis=0,
+                    )
+                    red.put(10 + 4 * half + sub, near % 2, b % 2, near // 2, b // 2, pair)
+
+    @pl.loop(10, 18)
+    def _(c):
+        red.start(c)
+
+    res[...] = jnp.zeros_like(res)
+
+    @pl.loop(0, 3)
+    def _(i):
+        @pl.loop(0, 2)
+        def _(h):
+            pair = 2 * i + h
+            grads = attend_pair_back(pair, length, proj, gmixed, lse_all)
+            for part in range(3):
+                gblk[:, pl.ds(pl.multiple_of(h * WIDE + part * 128, 128), 128)] = grads[part]
+            lanes = pl.ds(pl.multiple_of(pair * 128, 128), 128)
+            vecs[pl.ds(2, 1), lanes] = column_sum(grads[0].astype(F32))
+            vecs[pl.ds(3, 1), lanes] = column_sum(grads[2].astype(F32))
+
+            @pl.loop(0, 2)
+            def _(k):
+                red.tick(10 + 5 * i + 2 * h + k)
+
+        product[...] = dot(n1[...], gblk[...], 0, 0)
+        for half in range(2):
+            c = 18 + 2 * i + half
+            red.free(c)
+            red.place(c, half, product)
+            red.start(c)
+        red.tick(14 + 5 * i)
+        weights = jnp.concatenate(
+            [
+                wqkv[:, pl.ds(pl.multiple_of(part * width + (2 * i + h) * 128, 128), 128)]
+                for h in range(2)
+                for part in range(3)
+            ],
+            axis=1,
+        )
+        res[...] += dot(gblk[...], weights, 1, 1)
+
+    def first_back(b, totals):
+        at = pl.ds(pl.multiple_of(b * BLOCK, BLOCK), BLOCK)
+        normed, inverse = standardize(hidden[at])
+        upstream = res[at]
+        scaled = upstream * row(gain_one)
+        back = inverse * (scaled - mean(scaled) - normed * mean(scaled * normed))
+        grad = gn[at] + back
+        res[at] = grad
+        return (
+            totals[0] + fold(upstream * normed),
+            totals[1] + fold(upstream),
+            totals[2] + fold(grad),
+        )
+
+    totals = lax.fori_loop(0, blocks, first_back, (zero8, zero8, zero8))
+    vecs[pl.ds(0, 1)] = column_sum(totals[0])
+    vecs[pl.ds(1, 1)] = column_sum(totals[1])
+    strip_sum = column_sum(totals[2])
+    for group in range(table.shape[0]):
+        vecs[pl.ds(8 + group, 1)] = jnp.where(own_script == group, strip_sum, 0.0)
+    for j in range(strips):
+        cin[j] = res[pl.ds(j * row_count, row_count)].astype(BF)
+    from_grad = exchange(3, cin, grad_patches)
+    launch(from_grad)
+
+    held = (vecs, v1, v2, v3, v4, v5)
+    order = (dev.to_core, dev.to_x, dev.to_y, dev.to_low, dev.to_high)
+
+    def share_copy(stage):
+        return pltpu.make_async_remote_copy(
+            src_ref=held[stage],
+            dst_ref=held[stage + 1],
+            send_sem=vsend.at[stage],
+            recv_sem=vrecv.at[stage],
+            device_id=order[stage],
+            device_id_type=MESH,
+        )
+
+    share_copy(0).start()
+    done = 25
+    for stage in range(STAGES):
+        upto = CHUNKS + LAGS[min(stage, STAGES - 1)]
+
+        @pl.loop(done, upto)
+        def _(step):
+            red.tick(step)
+
+        done = max(done, upto)
+        share_copy(stage).wait_recv()
+        held[stage + 1][...] = held[stage + 1][...] + held[stage][...]
+        if stage + 1 < STAGES:
+            share_copy(stage + 1).start()
+
+    owner = s * strips + q
+    spread = lax.broadcasted_iota(jnp.int32, (width, 128), 0)
+    lane = lax.broadcasted_iota(jnp.int32, (width, 128), 1)
+    few = jnp.where((spread == PART * owner + lane) & (lane < PART), 1.0, 0.0)
+    many = jnp.where((spread == 4 * PART * (owner % 8) + lane) & (lane < 4 * PART), 1.0, 0.0)
+    exact = lambda left, right: lax.dot_general(
+        left, right, (((1,), (0,)), ((), ())), precision=lax.Precision.HIGHEST,
+        preferred_element_type=F32,
+    )
+    summed = v5[...]
+    lines = lax.broadcasted_iota(jnp.int32, (16, width), 0)
+    chosen = jnp.where(lines == 12 + owner // 8, summed, 0.0)
+    small[pl.ds(0, 16)] = exact(summed, few)
+    small[pl.ds(16, 16)] = exact(chosen, many)
+
+    red.finish()
+    for stage in range(STAGES):
+        share_copy(stage).wait_send()
+    for moves in (from_out, from_grad):
+        arrive(moves)
+    for moves in (into_x, into_c, from_out, from_grad):
+        for copy in moves[0]:
+            copy.wait_send()
+
+
+def run_layer(*arrays):
+    patches = arrays[12]
+    strips, row_count, width = patches.shape
+    rows = -(-strips * row_count // BLOCK) * BLOCK
+    hidden_units = arrays[16].shape[1]
+    vmem = pl.BlockSpec(memory_space=pltpu.VMEM)
+    smem = pl.BlockSpec(memory_space=pltpu.SMEM)
+    hbm = pl.BlockSpec(memory_space=pl.ANY)
+    packed = lambda *shape: pltpu.VMEM(shape, BF)
+    wide = lambda *shape: pltpu.VMEM(shape, F32)
+    return pl.pallas_call(
+        layer_kernel,
+        out_shape=[
+            jax.ShapeDtypeStruct(patches.shape, BF),
+            jax.ShapeDtypeStruct(patches.shape, BF),
+            jax.ShapeDtypeStruct((CHUNKS, PART, WIDE), F32),
+            jax.ShapeDtypeStruct((32, 128), F32),
+        ],
+        in_specs=[smem] * 2 + [vmem] * 10 + [hbm] * 6,
+        out_specs=[hbm, hbm, vmem, vmem],
+        scratch_shapes=[
+            packed(strips, row_count, width),
+            packed(strips, row_count, width),
+            wide(rows, width),
+            packed(rows, width),
+            packed(rows, 3 * width),
+            packed(rows, width),
+            wide(rows, 128),
+            wide(rows, width),
+            packed(rows, width),
+            packed(rows, hidden_units),
+            packed(rows, width),
+            wide(rows, width),
+            wide(rows, width),
+            packed(rows, width),
+            packed(rows, width),
+            packed(rows, width),
+            wide(width, width),
+            wide(8, width),
+            wide(16, width),
+            packed(width, 3 * width),
+            packed(width, width),
+            packed(2, width, width),
+            packed(2, width, width),
+            packed(SLOTS, 2, 384, WIDE),
+            packed(CHUNKS, 384, WIDE),
+            packed(CHUNKS, 192, WIDE),
+            packed(CHUNKS, 96, WIDE),
+            packed(CHUNKS, 48, WIDE),
+            wide(CHUNKS, 48, WIDE),
+            wide(CHUNKS, 24, WIDE),
+        ]
+        + [wide(16, width)] * STAGES
+        + [
+            pltpu.SemaphoreType.DMA((STAGES, CHUNKS)),
+            pltpu.SemaphoreType.DMA((STAGES, CHUNKS)),
+            pltpu.SemaphoreType.DMA((STAGES,)),
+            pltpu.SemaphoreType.DMA((STAGES,)),
+            pltpu.SemaphoreType.DMA((4, strips)),
+            pltpu.SemaphoreType.DMA((4, strips)),
+            pltpu.SemaphoreType.DMA((2,)),
+            pltpu.SemaphoreType.DMA((2, 2)),
+            pltpu.SemaphoreType.DMA((4,)),
+        ],
+        compiler_params=pltpu.CompilerParams(
+            collective_id=0, has_side_effects=True, vmem_limit_bytes=67043328
+        ),
+    )(*arrays)
+
+
+def finish_kernel(
+    layer_in, grad_in, reduced, small,
+    layer_out, grad_patches, table, gain_one, bias_one, qkv, query_bias, value_bias, out_weight,
+    out_bias, gain_two, bias_two, up_weight, up_bias, down_weight, down_bias,
+):
+    layer_out[...] = layer_in[...]
+    grad_patches[...] = grad_in[...]
+    names = (gain_one, bias_one, query_bias, value_bias, out_bias, gain_two, bias_two, down_bias)
+    for index, ref in enumerate(names):
+        ref[...] = small[pl.ds(index, 1), pl.ds(0, PART)].reshape(PART)
+    up_bias[...] = column_sum(small[pl.ds(16, 16), pl.ds(0, 4 * PART)]).reshape(4 * PART)
+    table[...] = small[pl.ds(8, 4), pl.ds(0, PART)].T
+    for c in range(8):
+        up_weight[:, pl.ds(c * WIDE, WIDE)] = reduced[c]
+    for c in range(2):
+        out_weight[:, pl.ds(c * WIDE, WIDE)] = reduced[8 + c]
+    for half in range(2):
+        for sub in range(4):
+            down_weight[pl.ds(sub * PART, PART), pl.ds(half * WIDE, WIDE)] = reduced[
+                10 + half * 4 + sub
+            ]
+    width = qkv.shape[1] // 3
+    for pair in range(6):
+        for part in range(3):
+            qkv[:, pl.ds(part * width + pair * 128, 128)] = reduced[
+                18 + pair, :, pl.ds(part * 128, 128)
+            ]
+
+
+def local(
+    patches,
+    lengths,
+    script,
+    script_table,
+    gain_one,
+    bias_one,
+    qkv_weight,
+    query_bias,
+    value_bias,
+    out_weight,
+    out_bias,
+    gain_two,
+    bias_two,
+    up_weight,
+    up_bias,
+    down_weight,
+    down_bias,
+    cotangent,
+):
+    strips, row_count, width = patches.shape
+    groups = script_table.shape[0]
+    results = run_layer(
+        lengths, script, script_table, gain_one, bias_one, query_bias, value_bias, out_bias,
+        gain_two, bias_two, up_bias.reshape(-1, width), down_bias, patches, cotangent, qkv_weight,
+        out_weight, up_weight, down_weight,
+    )
+    vector = jax.ShapeDtypeStruct((PART,), F32)
+    return pl.pallas_call(
+        finish_kernel,
+        out_shape=[
+            jax.ShapeDtypeStruct(patches.shape, BF),
+            jax.ShapeDtypeStruct(patches.shape, BF),
+            jax.ShapeDtypeStruct((PART, groups), F32),
+            vector,
+            vector,
+            jax.ShapeDtypeStruct((PART, 3 * width), F32),
+            vector,
+            vector,
+            jax.ShapeDtypeStruct((PART, width), F32),
+            vector,
+            vector,
+            vector,
+            jax.ShapeDtypeStruct((PART, up_weight.shape[1]), F32),
+            jax.ShapeDtypeStruct((4 * PART,), F32),
+            jax.ShapeDtypeStruct((4 * PART, width), F32),
+            vector,
+        ],
+    )(*results)
+
+
 def solution(mesh):
     placed = (
         P("strip", "seq", None),
@@ -229,8 +988,9 @@
         P(),
         P("strip", "seq", None),
     )
+    chosen = local if fits(mesh) else local_general
     return jax.shard_map(
-        local,
+        chosen,
         mesh=mesh,
         in_specs=placed,
         out_specs=(

time: 795 us -> 166 us (0.21); the launches traced: 786 us -> 165 us
  waiting for transfers between devices: 407 us -> 0 us
  Pallas kernels: 0 us -> 153 us
  local copies, waits for them, and re-layouts: 146 us -> 11.7 us
  matrix products: 116 us -> 0 us
  blocking collectives: 44.2 us -> 0 us
  other arithmetic: 39.8 us -> 0 us
  starting transfers between devices: 19 us -> 0 us
  between operations: 14.3 us -> 0.66 us
    reduce_scatter x4 -> x0, waiting for transfers between devices: 291 us -> none  [the longest x1 142 us: local(): lax.psum_scatter(grad_up_weight, ('strip', 'seq'), scatter_dimension=0, t...]
    pallas_call x0 -> x2, Pallas kernels: none -> 153 us  [the longest x1 150 us: run_layer(): pl.pallas_call(layer_kernel, out_shape=[jax.ShapeDtypeStruct(patches.shap...]
    dot_general x42 -> x0, matrix products: 116 us -> none  [the longest x4 32.1 us: weight_grad(): lax.dot_general(inputs, upstream, (((0,), (0,)), ((), ())), preferred_ele...]
    all_to_all x4 -> x0, waiting for transfers between devices: 115 us -> none  [the longest x1 54.5 us: local(): lax.all_to_all(projected, 'seq', split_axis=3, concat_axis=1, tiled=True)]
    reshape x11 -> x1, local copies, waits for them, and re-layouts: 46 us -> 1.32 us  [local(): up_bias.reshape(-1, width)]
    unnamed x1 -> x0, blocking collectives: 44.2 us -> none
    while x14 -> x0, local copies, waits for them, and re-layouts: 35.7 us -> none  [the longest x3 20.1 us: local(): mixed_heads, log_totals = lax.map(attend_forward, (head_blocks, lengths))]
    unnamed x67 -> x2, local copies, waits for them, and re-layouts: 24 us -> 4.28 us
  transfers between devices with their start and end apart: 8 -> 0, of which waited for: 7 -> 0; matrix products, arithmetic and copies ran while one was open for 21% -> 0% of each run, Pallas kernels for 0% -> 0%
where the time goes in v2:
time: 166 us; the launch traced here: 165 us
  Pallas kernels  153 us (92%)
  local copies, waits for them, and re-layouts  11.7 us (7%)
    pallas_call x1, Pallas kernels, run_layer(): pl.pallas_call(layer_kernel, out_shape=[jax.ShapeDtypeStruct(patches.shap...  150 us
    pallas_call x3, local copies, waits for them, and re-layouts, local(): pl.pallas_call(finish_kernel, out_shape=[jax.ShapeDtypeStruct(patches.sha...  6.07 us
    unnamed x2, local copies, waits for them, and re-layouts  4.28 us

profile of v2, /device:TPU:0, one launch (start us, length us, event | category | flops | bytes accessed | tf_op | source)
XLA Modules:
  0.0 165.3 jit_solution(13260031436613534049)
XLA Ops:
  0.6 1.3 reshape.35.up_bias
  2.0 2.1 %copy.34.patches = bf16[4,134,768]{2,1,0:T(8,128)(2,1)} copy(bf16[4,134,768]{2,0,1:T(4,128)(2,1)} %param.18) | data formatting | bytes 1646592 | tf_op args[0]
  4.1 2.2 %copy.35.cotangent = bf16[4,134,768]{2,1,0:T(8,128)(2,1)} copy(bf16[4,134,768]{2,0,1:T(4,128)(2,1)} %param.35) | data formatting | bytes 1646592 | tf_op args[17]
  6.2 149.7 %shard_map.297 = (bf16[4,134,768]{2,1,0:T(8,128)(2,1)}, bf16[4,134,768]{2,1,0:T(8,128)(2,1)}, f32[24,24,384]{2,1,0:T(8,128)}, f32[32,128]{1,0:T(8,128)}) custom-call(s32[4]{0:T(128)} %lengths.1, s32[4]{0:T(128)} %script.1, bf16[4,768]{1,0:T(4,128)(2,1)} %table.1, f32[768]{0:T(1024)} %gain_one.1, f32[768]{0:T(1024)} %bias_one.1, f32[768]{0:T(1024)} %query_bias.1, ...), custom_call_target="tpu_custom_call" | custom-call | tf_op jit(solution)/shard_map/pallas_call | solution.py:830
  156.0 3.2 %shard_map.298 = (bf16[4,134,768]{2,1,0:T(8,128)(2,1)}, bf16[4,134,768]{2,1,0:T(8,128)(2,1)}, f32[24,4]{1,0:T(8,128)}, f32[24]{0:T(128)}, f32[24]{0:T(128)}, /*i...) custom-call(bf16[4,134,768]{2,1,0:T(8,128)(2,1)} %get-tuple-element., ...), custom_call_target="tpu_custom_call" | custom-call | tf_op jit(solution)/shard_map/pallas_call | solution.py:947
  159.2 2.4 %copy.36 = bf16[4,134,768]{2,0,1:T(4,128)(2,1)} copy(bf16[4,134,768]{2,1,0:T(8,128)(2,1)} %get-tuple-element.24) | data formatting | bytes 1646592 | tf_op jit(solution)/shard_map/pallas_call | solution.py:947
  161.6 1.4 copy.38
  163.0 2.4 %copy.37 = bf16[4,134,768]{2,0,1:T(4,128)(2,1)} copy(bf16[4,134,768]{2,1,0:T(8,128)(2,1)} %get-tuple-element.25) | data formatting | bytes 1646592 | tf_op jit(solution)/shard_map/pallas_call | solution.py:947
